TPU v7x, 8 devices: a whole 2x2x1 slice. The times are simulated.
8 devices in a mesh: dp: 1 (over z), sp: 2 (over y), tp: 4 (over x, core).
Axes of the slice: x: 2, y: 2, z: 1, core: 2. Of those that a mesh axis runs over, the one named last changes fastest.
Arguments:
- x_seq: bfloat16 [2, 512, 8192], P('dp', ('sp', 'tp'))
- w_zx: bfloat16 [8192, 2, 16384], P(None, None, 'tp')
- w_dt: bfloat16 [8192, 256], P(None, 'tp')
- w_bc: bfloat16 [8192, 2, 8, 256], replicated
- conv_x: bfloat16 [4, 16384], P(None, 'tp')
- conv_bc: bfloat16 [4, 2, 8, 256], replicated
- bias_x: bfloat16 [16384], P('tp')
- bias_bc: bfloat16 [2, 8, 256], replicated
- a_log: float32 [256], P('tp')
- dt_bias: float32 [256], P('tp')
- d_skip: float32 [256], P('tp')
- norm_w: bfloat16 [16384], P('tp')
- w_out: bfloat16 [16384, 8192], P('tp')
Outputs:
- output: bfloat16 [2, 512, 8192], P('dp', ('sp', 'tp'))
All inputs are finite; a program needn't handle non-finite values.
Results may differ from a plain program's by a relative error of at most 0.00554757.
Values are sent between devices in bfloat16 or wider.
A program may use at most 1.25 GiB of HBM per device.

v0:
```python
import jax
import jax.numpy as jnp
from jax import lax
from jax.sharding import PartitionSpec as P

TILE = 256


def causal_conv(pre_conv, halo_rows, conv_w, conv_b):
    length = pre_conv.shape[1]
    padded = jnp.concatenate([halo_rows, pre_conv], axis=1)
    conv_sum = conv_b.astype(jnp.float32)
    for tap_idx in range(conv_w.shape[0]):
        conv_sum = conv_sum + padded[:, tap_idx:tap_idx + length].astype(jnp.float32) * conv_w[tap_idx].astype(jnp.float32)
    return jax.nn.silu(conv_sum).astype(jnp.bfloat16)


def ssd_block(x_heads, b_mat, c_mat, dt_vals, log_a, tile_len):
    n_seq, length = x_heads.shape[0], x_heads.shape[1]
    n_tiles = length // tile_len

    def to_tiles(array_in):
        return jnp.moveaxis(array_in.reshape((n_seq, n_tiles, tile_len) + array_in.shape[2:]), 1, 0)

    cum_in = jnp.cumsum(to_tiles(log_a), axis=2)
    tile_tot = cum_in[:, :, -1]
    offsets = jnp.cumsum(tile_tot, axis=0) - tile_tot
    cum_block = jnp.moveaxis(cum_in + offsets[:, :, None], 0, 1).reshape(log_a.shape)
    causal = (jnp.arange(tile_len)[:, None] >= jnp.arange(tile_len)[None, :])[None, :, :, None, None]

    def tile_step(carry_state, tile_in):
        x_part, b_part, c_part, dt_part, cum_part = tile_in
        x_f32 = x_part.astype(jnp.float32)
        scores = jnp.einsum('atgn,asgn->atsg', c_part, b_part, preferred_element_type=jnp.float32)
        log_diff = cum_part[:, :, None] - cum_part[:, None, :]
        decay_mat = jnp.where(causal, jnp.exp(jnp.where(causal, log_diff, 0.0)), 0.0)
        weights = scores[..., None] * decay_mat * dt_part[:, None]
        y_diag = jnp.einsum('atsgk,asgkp->atgkp', weights, x_f32)
        y_prev = jnp.einsum('atgn,agkpn->atgkp', c_part.astype(jnp.float32), carry_state) * jnp.exp(cum_part)[..., None]
        tile_end = cum_part[:, -1]
        weighted_x = x_f32 * (jnp.exp(tile_end[:, None] - cum_part) * dt_part)[..., None]
        new_state = jnp.exp(tile_end)[..., None, None] * carry_state + jnp.einsum('asgkp,asgn->agkpn', weighted_x, b_part.astype(jnp.float32))
        return new_state, y_diag + y_prev

    zero_state = jnp.zeros((n_seq,) + x_heads.shape[2:] + (b_mat.shape[-1],), jnp.float32)
    end_state, y_tiles = lax.scan(tile_step, zero_state, (to_tiles(x_heads), to_tiles(b_mat), to_tiles(c_mat), to_tiles(dt_vals), cum_in))
    y_ssd = jnp.moveaxis(y_tiles, 0, 1).reshape(x_heads.shape)
    return y_ssd, end_state, cum_block, jnp.sum(tile_tot, axis=0)


def solution(mesh):
    sp_size = mesh.shape['sp']
    tp_size = mesh.shape['tp']
    tok_spec = P('dp', ('sp', 'tp'), None)
    fwd_pairs = [(sender, sender + 1) for sender in range(sp_size - 1)]

    def local_layer(x_loc, w_zx, w_dt, w_bc, conv_x, conv_bc, bias_x, bias_bc, a_log, dt_bias, d_skip, norm_w, w_out):
        n_seq = x_loc.shape[0]
        groups = w_bc.shape[2]
        heads_loc = a_log.shape[0]
        inner_loc = w_zx.shape[2]
        head_dim = inner_loc // heads_loc
        groups_loc = max(groups // tp_size, 1)
        per_group = heads_loc // groups_loc
        tp_idx = lax.axis_index('tp')
        group_first = (tp_idx * groups) // tp_size
        w_bc_loc = lax.dynamic_slice_in_dim(w_bc, group_first, groups_loc, axis=2)
        conv_bc_loc = lax.dynamic_slice_in_dim(conv_bc, group_first, groups_loc, axis=2)
        bias_bc_loc = lax.dynamic_slice_in_dim(bias_bc, group_first, groups_loc, axis=1)

        x_blk = lax.all_gather(x_loc, 'tp', axis=1, tiled=True)
        blk_len = x_blk.shape[1]
        zx_out = jnp.einsum('ald,dce->cale', x_blk, w_zx, preferred_element_type=jnp.float32).astype(jnp.bfloat16)
        bc_pre = jnp.einsum('ald,dcgn->alcgn', x_blk, w_bc_loc, preferred_element_type=jnp.float32).astype(jnp.bfloat16)
        dt_raw = jnp.einsum('ald,dh->alh', x_blk, w_dt, preferred_element_type=jnp.float32).astype(jnp.bfloat16)

        x_halo = lax.ppermute(zx_out[1][:, -3:], 'sp', fwd_pairs)
        bc_halo = lax.ppermute(bc_pre[:, -3:], 'sp', fwd_pairs)
        x_act = causal_conv(zx_out[1], x_halo, conv_x, bias_x)
        bc_act = causal_conv(bc_pre, bc_halo, conv_bc_loc, bias_bc_loc)

        hd_shape = (n_seq, blk_len, groups_loc, per_group)
        dt_vals = jax.nn.softplus(dt_raw.astype(jnp.float32) + dt_bias)
        log_a = -jnp.exp(a_log) * dt_vals
        x_heads = x_act.reshape(hd_shape + (head_dim,))
        c_mat = bc_act[:, :, 1]
        y_ssd, end_state, cum_block, total_log = ssd_block(x_heads, bc_act[:, :, 0], c_mat, dt_vals.reshape(hd_shape), log_a.reshape(hd_shape), TILE)

        block_decay = jnp.exp(total_log)[..., None, None]

        def chain_hop(hop_idx, incoming):
            return lax.ppermute(block_decay * incoming + end_state, 'sp', fwd_pairs)

        state_in = lax.fori_loop(0, sp_size - 1, chain_hop, jnp.zeros_like(end_state))
        y_ssd = y_ssd + jnp.exp(cum_block)[..., None] * jnp.einsum('atgn,agkpn->atgkp', c_mat.astype(jnp.float32), state_in)
        y_ssd = y_ssd + d_skip.reshape(groups_loc, per_group, 1) * x_heads.astype(jnp.float32)
        gated_y = y_ssd.reshape(n_seq, blk_len, inner_loc) * jax.nn.silu(zx_out[0].astype(jnp.float32))
        if groups >= tp_size:
            grouped = gated_y.reshape(n_seq, blk_len, groups_loc, inner_loc // groups_loc)
            inv_rms = lax.rsqrt(jnp.mean(jnp.square(grouped), axis=-1, keepdims=True) + 1e-5)
            normed = (grouped * inv_rms).reshape(n_seq, blk_len, inner_loc)
        else:
            group_size = inner_loc * tp_size // groups
            one_hot = (jnp.arange(groups) == group_first).astype(jnp.float32)
            sq_part = jnp.sum(jnp.square(gated_y), axis=-1, keepdims=True) * one_hot
            sq_total = jnp.sum(lax.psum(sq_part, 'tp') * one_hot, axis=-1, keepdims=True)
            normed = gated_y * lax.rsqrt(sq_total / group_size + 1e-5)
        normed = (normed * norm_w.astype(jnp.float32)).astype(jnp.bfloat16)
        out_part = jnp.einsum('ale,ed->ald', normed, w_out, preferred_element_type=jnp.float32)
        out_loc = lax.psum_scatter(out_part, 'tp', scatter_dimension=1, tiled=True)
        return (x_loc.astype(jnp.float32) + out_loc).astype(jnp.bfloat16)

    in_specs = (tok_spec, P(None, None, 'tp'), P(None, 'tp'), P(), P(None, 'tp'), P(), P('tp'), P(), P('tp'), P('tp'), P('tp'), P('tp'), P('tp', None))
    return jax.shard_map(local_layer, mesh=mesh, in_specs=in_specs, out_specs=tok_spec, check_vma=False)
```

profile of v0, /device:TPU:0, one launch (start us, length us, event | category | flops | bytes accessed | tf_op | source)
XLA Modules:
  0.0 509.4 jit_solution(7200615620114734030)
XLA Ops:
  7.3 1.3 convert_element_type.171
  8.6 1.3 dynamic-slice_convert_fusion
  9.9 1.4 fusion.60
  11.9 1.6 slice_convert_fusion.4
  13.5 27.2 %constant_dynamic-slice_fusion = bf16[8192,2,2,256]{3,2,1,0:T(2,128)(2,1)} fusion(bf16[8192,2,8,256]{3,2,1,0:T(8,128)(2,1)} %param.16, s32[]{:T(128)S(6)} %select_n.24), kind=kLoop, calls=%fused_computation.103 | loop fusion | bytes 33554436 | tf_op jit(solution)/shard_map/dynamic_slice | solution.py:67
  40.7 26.7 %all-gather.2.cloned.1.call-done = bf16[2,256,8192]{2,1,0:T(8,128)(2,1)} async-done(((bf16[2,64,8192]{2,1,0:T(8,128)(2,1)}), bf16[2,256,8192]{2,1,0:T(8,128)(2,1)}) %all-gather.2.cloned.1.call-update) | async-done | bytes 8388624 | tf_op jit(solution)/shard_map/all_gather | solution.py:71
  67.5 6.8 %broadcast_multiply_fusion = (f32[2,256,64]{1,2,0:T(8,128)S(1)}, f32[2,256,64]{1,2,0:T(8,128)}) fusion(f32[64]{0:T(128)S(1)} %exponential_negate_fusion, f32[64]{0:T(128)S(1)} %copy-done.23, bf16[2,256,8192]{2,1,0:T(8,128)(2,1)} %all-gather.2.cloned.1.call-done, bf16[8192,64]{0,1:T(8,128)(2,1)S(1)} %copy-done), kind=kOutput, calls=%fused_computation.83 | convolution fusion | flops 537198592 | bytes 9699840 | tf_op jit(solution)/shard_map/ald,dh->alh/dot_general | solution.py:75
  74.4 2.3 reduce-window.6
  77.5 1.3 fusion.63
  80.0 1.1 add_bitcast_fusion.1
  81.0 14.9 %fusion.42 = bf16[2,256,2,2,256]{4,1,0,3,2:T(8,128)(2,1)S(1)} fusion(bf16[2,256,8192]{2,1,0:T(8,128)(2,1)} %all-gather.2.cloned.1.call-done, bf16[8192,2,2,256]{3,2,1,0:T(2,128)(2,1)} %constant_dynamic-slice_fusion), kind=kOutput, calls=%fused_computation.60 | convolution fusion | flops 8590458880 | bytes 26214400 | tf_op jit(solution)/shard_map/ald,dcgn->alcgn/dot_general | solution.py:74
  96.6 3.5 collective-permute-start.1
  100.1 80.4 %convert_bitcast_fusion = bf16[2,2,256,4096]{2,3,1,0:T(8,128)(2,1)} fusion(bf16[2,256,8192]{2,1,0:T(8,128)(2,1)} %all-gather.2.cloned.1.call-done, bf16[8192,2,4096,1]{2,1,0,3:T(2,128)(2,1)} %bitcast), kind=kOutput, calls=%fused_computation.41 | convolution fusion | flops 68723671040 | bytes 150994944 | tf_op jit(solution)/shard_map/ald,dce->cale/dot_general | solution.py:73
  180.6 6.0 %slice_convert_fusion = (f32[1,2,256,4096]{2,3,1,0:T(8,128)}, bf16[2,256,4096]{1,2,0:T(8,128)(2,1)S(1)}) fusion(bf16[2,2,256,4096]{2,3,1,0:T(8,128)(2,1)} %convert_bitcast_fusion), kind=kLoop, calls=%fused_computation.48 | loop fusion | flops 2097152 | bytes 20971520 | tf_op jit(solution)/shard_map/convert_element_type | solution.py:97
  186.6 1.9 copy-done.2
  189.2 0.9 copy.99
  190.1 1.9 collective-permute-start
  193.4 4.2 multiply_convert_fusion.1
  197.7 1.4 slice_bitcast_fusion.3
  199.0 1.8 copy.100
  200.9 12.7 %multiply_convert_fusion = bf16[2,256,4096]{1,2,0:T(8,128)(2,1)S(1)} fusion(bf16[2,256,4096]{1,2,0:T(8,128)(2,1)} %copy-done.2, bf16[2,3,4096]{1,2,0:T(8,128)(2,1)S(1)} %copy.100, f32[4096]{0:T(1024)S(1)} %bitcast.163, f32[4096]{0:T(1024)S(1)} %bitcast.164, f32[4096]{0:T(1024)S(1)} %bitcast.162, f32[4096]{0:T(1024)S(1)} %bitcast.161, f32[4096]{0:T(1024)S(1)} %copy-done.17), kind=kLoop, calls=%fused_computation.40 | loop fusion | flops 54525952 | bytes 8519680 | tf_op jit(solution)/shard_map/convert_element_type | solution.py:15
  213.7 2.0 copy-done.6
  215.7 3.0 add_add_fusion
  218.7 3.5 collective-permute-start.2
  225.7 5.5 %fusion.37 = f32[2,2,32,64,256]{4,3,2,1,0:T(8,128)} fusion(bf16[2,256,2,256,1]{3,1,0,2,4:T(8,128)(2,1)S(1)} %copy-done.10), kind=kOutput, calls=%fused_computation.53 | convolution fusion | flops 1073741824 | bytes 8912896 | tf_op jit(solution)/shard_map/while/body/eval_jaxpr/atgn,agkpn->atgkp/dot_general | solution.py:39
  231.2 12.1 %fusion.4 = f32[2,2,32,64,256]{4,3,2,1,0:T(8,128)} fusion(bf16[2,256,2,32,64]{1,4,3,2,0:T(8,128)(2,1)S(1)} %bitcast.155, f32[2,256,2,32]{1,3,2,0:T(8,128)S(1)} %bitcast.157, f32[2,256,2,32]{1,3,2,0:T(8,128)S(1)} %copy-done.16, f32[2,256,256,2]{2,1,3,0:T(8,128)S(1)} %copy.104, pred[256,256]{1,0:T(8,128)(4,1)S(1)} %copy-done.22), kind=kOutput, calls=%fused_computation.4 | convolution fusion | flops 1115684864 | bytes 13959168 | tf_op jit(solution)/shard_map/while/body/eval_jaxpr/atsgk,asgkp->atgkp/dot_general | solution.py:38
  243.3 66.9 %collective-permute-done.2 = bf16[2,2,32,64,256]{4,3,2,1,0:T(8,128)(2,1)} collective-permute-done((bf16[2,2,32,64,256]{4,3,2,1,0:T(8,128)(2,1)}, bf16[2,2,32,64,256]{4,3,2,1,0:T(8,128)(2,1)}, u32[]{:S(2)}, u32[]{:S(2)}) %collective-permute-start.2) | collective-permute-done | bytes 4194336 | tf_op jit(solution)/shard_map/while/body/eval_jaxpr/ppermute | solution.py:92
  310.2 16.4 %multiply_reduce_fusion = (f32[2,256,2]{1,2,0:T(2,128)S(1)}, f32[2,256,2,32,64]{1,4,3,2,0:T(8,128)}) fusion(f32[2,256,2,32,64]{1,4,3,2,0:T(8,128)} %bitcast.150, bf16[2,256,2,32,64]{1,4,3,2,0:T(8,128)(2,1)} %bitcast.154, f32[2,32]{1,0:T(2,128)S(1)} %copy-done.30, bf16[2,2,32,64,256]{4,3,2,1,0:T(8,128)(2,1)} %collective-permute-done.2, ...), kind=kOutput, calls=%fused_computation.38 | convolution fusion | flops 1103100928 | bytes 42733824 | tf_op jit(solution)/shard_map/atgn,agkpn->atgkp/dot_general | solution.py:95
  326.6 6.4 %fusion.22 = bf16[2,256,4096]{1,2,0:T(8,128)(2,1)} fusion(f32[2,256,2,32,64]{1,4,3,2,0:T(8,128)} %get-tuple-element.65, f32[4096]{0:T(1024)S(1)} %convert_element_type.210, f32[2,256,2]{1,2,0:T(2,128)S(1)} %add_rsqrt_fusion, bf16[2,2,256,4096]{2,3,1,0:T(8,128)(2,1)S(1)} %bitcast.149), kind=kLoop, calls=%fused_computation.26 | loop fusion | flops 18874368 | bytes 16797696 | tf_op jit(solution)/shard_map/convert_element_type | solution.py:108
  333.1 45.2 %fusion.2 = f32[2,256,8192]{2,1,0:T(8,128)} fusion(bf16[2,256,4096]{1,2,0:T(8,128)(2,1)} %fusion.22, bf16[4096,8192]{1,0:T(8,128)(2,1)} %param.25), kind=kOutput, calls=%fused_computation.2 | convolution fusion | flops 34359738368 | bytes 88080384 | tf_op jit(solution)/shard_map/ale,ed->ald/dot_general | solution.py:109
  378.3 119.9 %reduce-scatter.2.cloned.1.call-done = f32[2,64,8192]{2,1,0:T(8,128)} async-done(((f32[2,256,8192]{2,1,0:T(8,128)}), f32[2,64,8192]{2,1,0:T(8,128)}) %reduce-scatter.2.cloned.1.call-update) | async-done | bytes 4194320 | tf_op jit(solution)/shard_map/reduce_scatter | solution.py:110
  498.2 3.9 add_convert_fusion
  (100 shorter events, 9.7 us)
Async XLA Ops:
  6.5 60.9 %copy-start = (bf16[8192,64]{0,1:T(8,128)(2,1)S(1)}, bf16[8192,64]{0,1:T(8,128)(2,1)}, u32[]{:S(2)}) copy-start(bf16[8192,64]{0,1:T(8,128)(2,1)} %param.15) | copy-start | bytes 3145732
  6.5 60.9 %all-gather.2.cloned.1.call-start = ((), (), s32[]{:S(2)}) async-start(), calls=%async_computation.1 | async-start | bytes 10485760 | tf_op jit(solution)/shard_map/all_gather | solution.py:71
  7.3 491.0 %reduce-scatter.2.cloned.1.call-start = ((), (), s32[]{:S(2)}) async-start(), calls=%async_computation.2 | async-start | bytes 20971520 | tf_op jit(solution)/shard_map/reduce_scatter | solution.py:110
  13.5 53.9 %copy-start.23 = (f32[64]{0:T(128)S(1)}, f32[64]{0:T(128)}, u32[]{:S(2)}) copy-start(f32[64]{0:T(128)} %param.22) | copy-start | bytes 772
  78.8 17.1 %copy-start.4 = (f32[2,256,2,32]{3,2,1,0:T(2,128)}, f32[2,256,2,32]{3,2,1,0:T(2,128)S(1)}, u32[]{:S(2)}) copy-start(f32[2,256,2,32]{3,2,1,0:T(2,128)S(1)} %get-tuple-element.26) | copy-start | bytes 393220
  95.9 84.6 %copy-start.13 = (bf16[2,256,2,2,256]{4,1,0,3,2:T(8,128)(2,1)}, bf16[2,256,2,2,256]{4,1,0,3,2:T(8,128)(2,1)S(1)}, u32[]{:S(2)}) copy-start(bf16[2,256,2,2,256]{4,1,0,3,2:T(8,128)(2,1)S(1)} %fusion.42) | copy-start | bytes 3145732
  96.6 96.9 %collective-permute-start.1 = (bf16[2,3,2,2,256]{4,1,0,3,2:T(4,128)(2,1)}, bf16[2,3,2,2,256]{4,1,0,3,2:T(4,128)(2,1)S(1)}, u32[]{:S(2)}, u32[]{:S(2)}) collective-permute-start(bf16[2,3,2,2,256]{4,1,0,3,2:T(4,128)(2,1)} %slice.104), channel_id=1, source_target_pairs={{0,4},{1,5},{2,6},{3,7}} | collective-permute-start | bytes 36872 | tf_op jit(solution)/shard_map/ppermute | solution.py:78
  180.5 11.5 %copy-start.14 = (f32[2,256,64]{1,2,0:T(8,128)S(1)}, f32[2,256,64]{1,2,0:T(8,128)}, u32[]{:S(2)}) copy-start(f32[2,256,64]{1,2,0:T(8,128)} %get-tuple-element.63) | copy-start | bytes 393220
  180.5 11.7 %copy-start.8 = (f32[1,2,256,2,32]{4,3,2,1,0:T(2,128)S(1)}, f32[1,2,256,2,32]{4,3,2,1,0:T(2,128)}, u32[]{:S(2)}) copy-start(f32[1,2,256,2,32]{4,3,2,1,0:T(2,128)} %add_bitcast_fusion.1) | copy-start | bytes 393220
  180.5 12.3 %copy-start.5 = (f32[2,256,2,32]{3,2,1,0:T(2,128)S(1)}, f32[2,256,2,32]{3,2,1,0:T(2,128)}, u32[]{:S(2)}) copy-start(f32[2,256,2,32]{3,2,1,0:T(2,128)} %copy-done.4) | copy-start | bytes 393220
  180.6 12.3 %copy-start.25 = (f32[2,2,32]{2,1,0:T(2,128)S(1)}, f32[2,2,32]{2,1,0:T(2,128)}, u32[]{:S(2)}) copy-start(f32[2,2,32]{2,1,0:T(2,128)} %slice_bitcast_fusion.6) | copy-start | bytes 1540
  186.6 14.3 %copy-start.17 = (f32[4096]{0:T(1024)S(1)}, f32[4096]{0:T(1024)}, u32[]{:S(2)}) copy-start(f32[4096]{0:T(1024)} %convert_element_type.171) | copy-start | bytes 49156
  186.6 14.3 %copy-start.18 = (f32[1,4096]{1,0:T(1,128)S(1)}, f32[1,4096]{1,0:T(1,128)}, u32[]{:S(2)}) copy-start(f32[1,4096]{1,0:T(1,128)} %get-tuple-element.58) | copy-start | bytes 49156
  186.6 14.3 %copy-start.19 = (f32[1,4096]{1,0:T(1,128)S(1)}, f32[1,4096]{1,0:T(1,128)}, u32[]{:S(2)}) copy-start(f32[1,4096]{1,0:T(1,128)} %get-tuple-element.59) | copy-start | bytes 49156
  186.6 14.3 %copy-start.20 = (f32[1,4096]{1,0:T(1,128)S(1)}, f32[1,4096]{1,0:T(1,128)}, u32[]{:S(2)}) copy-start(f32[1,4096]{1,0:T(1,128)} %get-tuple-element.60) | copy-start | bytes 49156
  186.6 14.3 %copy-start.21 = (f32[1,4096]{1,0:T(1,128)S(1)}, f32[1,4096]{1,0:T(1,128)}, u32[]{:S(2)}) copy-start(f32[1,4096]{1,0:T(1,128)} %get-tuple-element.61) | copy-start | bytes 49156
  190.1 8.9 %collective-permute-start = (bf16[2,3,4096]{2,0,1:T(2,128)(2,1)S(1)}, bf16[2,3,4096]{2,0,1:T(2,128)(2,1)}, u32[]{:S(2)}, u32[]{:S(2)}) collective-permute-start(bf16[2,3,4096]{2,0,1:T(2,128)(2,1)S(1)} %copy.99), channel_id=1, source_target_pairs={{0,4},{1,5},{2,6},{3,7}} | collective-permute-start | bytes 147464 | tf_op jit(solution)/shard_map/ppermute | solution.py:77
  197.6 18.0 %copy-start.27 = (f32[2,2,32]{2,1,0:T(2,128)S(1)}, f32[2,2,32]{2,1,0:T(2,128)}, u32[]{:S(2)}) copy-start(f32[2,2,32]{2,1,0:T(2,128)} %get-tuple-element.46) | copy-start | bytes 1540
  197.7 18.0 %copy-start.28 = (f32[2,2,32]{2,1,0:T(2,128)S(1)}, f32[2,2,32]{2,1,0:T(2,128)}, u32[]{:S(2)}) copy-start(f32[2,2,32]{2,1,0:T(2,128)} %exponential_multiply_fusion.1) | copy-start | bytes 1540
  200.8 14.9 %copy-start.15 = (bf16[2,256,2,256,1]{3,1,0,2,4:T(8,128)(2,1)S(1)}, bf16[2,256,2,256,1]{3,1,0,2,4:T(8,128)(2,1)}, u32[]{:S(2)}) copy-start(bf16[2,256,2,256,1]{3,1,0,2,4:T(8,128)(2,1)} %get-tuple-element.38) | copy-start | bytes 1572868
  213.6 9.1 %copy-start.26 = (bf16[4096]{0:T(1024)(128)(2,1)S(1)}, bf16[4096]{0:T(1024)(128)(2,1)}, u32[]{:S(2)}) copy-start(bf16[4096]{0:T(1024)(128)(2,1)} %param.24) | copy-start | bytes 24580
  213.7 10.6 %copy-start.24 = (f32[2,2,32]{2,1,0:T(2,128)S(1)}, f32[2,2,32]{2,1,0:T(2,128)}, u32[]{:S(2)}) copy-start(f32[2,2,32]{2,1,0:T(2,128)} %get-tuple-element.47) | copy-start | bytes 1540
  213.7 11.1 %copy-start.9 = (f32[2,256,2,32]{3,2,1,0:T(2,128)S(1)}, f32[2,256,2,32]{3,2,1,0:T(2,128)}, u32[]{:S(2)}) copy-start(f32[2,256,2,32]{3,2,1,0:T(2,128)} %get-tuple-element.25) | copy-start | bytes 393220
  213.7 11.2 %copy-start.11 = (bf16[2,256,2,256]{3,1,0,2:T(8,128)(2,1)S(1)}, bf16[2,256,2,256]{3,1,0,2:T(8,128)(2,1)}, u32[]{:S(2)}) copy-start(bf16[2,256,2,256]{3,1,0,2:T(8,128)(2,1)} %get-tuple-element.44) | copy-start | bytes 1572868
  213.7 11.2 %copy-start.12 = (bf16[2,256,2,256]{3,1,0,2:T(8,128)(2,1)S(1)}, bf16[2,256,2,256]{3,1,0,2:T(8,128)(2,1)}, u32[]{:S(2)}) copy-start(bf16[2,256,2,256]{3,1,0,2:T(8,128)(2,1)} %get-tuple-element.45) | copy-start | bytes 1572868
  215.7 10.0 %copy-start.10 = (bf16[2,256,2,256,1]{3,1,0,2,4:T(8,128)(2,1)S(1)}, bf16[2,256,2,256,1]{3,1,0,2,4:T(8,128)(2,1)}, u32[]{:S(2)}) copy-start(bf16[2,256,2,256,1]{3,1,0,2,4:T(8,128)(2,1)} %get-tuple-element.39) | copy-start | bytes 1572868
  218.7 91.5 %collective-permute-start.2 = (bf16[2,2,32,64,256]{4,3,2,1,0:T(8,128)(2,1)}, bf16[2,2,32,64,256]{4,3,2,1,0:T(8,128)(2,1)}, u32[]{:S(2)}, u32[]{:S(2)}) collective-permute-start(bf16[2,2,32,64,256]{4,3,2,1,0:T(8,128)(2,1)} %add_add_fusion), channel_id=1, source_target_pairs={{0,4},{1,5},{2,6},{3,7}} | collective-permute-start | bytes 12582920 | tf_op jit(solution)/shard_map/while/body/eval_jaxpr/ppermute | solution.py:92
  225.7 101.0 %slice-start = ((s8[8388608]{0:T(1024)(128)(4,1)}), s8[4194304]{0:T(1024)(128)(4,1)S(1)}, s32[]{:S(2)}) async-start(s8[8388608]{0:T(1024)(128)(4,1)} %bitcast.148), calls=%async_computation.3 | async-start | bytes 8388608
  231.1 79.0 %copy-start.30 = (f32[2,32]{1,0:T(2,128)S(1)}, f32[2,32]{1,0:T(2,128)}, u32[]{:S(2)}) copy-start(f32[2,32]{1,0:T(2,128)} %mul.261) | copy-start | bytes 772
  231.1 95.5 %slice-start.1 = ((s8[8388608]{0:T(1024)(128)(4,1)}), s8[4194304]{0:T(1024)(128)(4,1)S(1)}, s32[]{:S(2)}) async-start(s8[8388608]{0:T(1024)(128)(4,1)} %bitcast.148), calls=%async_computation.4 | async-start | bytes 8388608
  378.3 119.9 %copy-start.3 = (bf16[2,64,8192]{2,1,0:T(8,128)(2,1)S(1)}, bf16[2,64,8192]{2,1,0:T(8,128)(2,1)}, u32[]{:S(2)}) copy-start(bf16[2,64,8192]{2,1,0:T(8,128)(2,1)} %param.13) | copy-start | bytes 6291460
  378.3 123.8 %copy-start.1 = (bf16[8192,64]{0,1:T(8,128)(2,1)S(1)}, bf16[8192,64]{0,1:T(8,128)(2,1)}, u32[]{:S(2)}) copy-start(bf16[8192,64]{0,1:T(8,128)(2,1)} %param.15) | copy-start | bytes 3145732
  (6 other events, 29.8 us)
Sparse Core Ops, SparseCore 0:
  8.9 58.5 all-gather.1
  378.4 119.7 reduce-scatter.1
where the time goes:
time: 517 us; the launch traced here: 509 us
  waiting for transfers between devices  214 us (41%)
  matrix products  185 us (36%)
  other arithmetic  46.7 us (9%)
  local copies, waits for them, and re-layouts  40.6 us (8%)
  between operations  14.3 us (3%)
  starting transfers between devices  8.96 us (2%)
    reduce_scatter x1, waiting for transfers between devices, local_layer(): out_loc = lax.psum_scatter(out_part, 'tp', scatter_dimension=1, tiled=True)  120 us
    dot_general x1, matrix products, local_layer(): jnp.einsum('ald,dce->cale', x_blk, w_zx, preferred_element_type=jnp.float32)  80.4 us
    ppermute x1, waiting for transfers between devices, chain_hop(): return lax.ppermute(block_decay * incoming + end_state, 'sp', fwd_pairs)  66.9 us
    dot_general x1, matrix products, local_layer(): jnp.einsum('ale,ed->ald', normed, w_out, preferred_element_type=jnp.float32)  45.2 us
    dynamic_slice x1, local copies, waits for them, and re-layouts, local_layer(): w_bc_loc = lax.dynamic_slice_in_dim(w_bc, group_first, groups_loc, axis=2)  27.2 us
    all_gather x1, waiting for transfers between devices, local_layer(): x_blk = lax.all_gather(x_loc, 'tp', axis=1, tiled=True)  26.7 us
    convert_element_type x2, other arithmetic, causal_conv(): return jax.nn.silu(conv_sum).astype(jnp.bfloat16)  16.9 us
    dot_general x1, matrix products, local_layer(): jnp.einsum('atgn,agkpn->atgkp', c_mat.astype(jnp.float32), state_in)  16.4 us
  transfers between devices with their start and end apart: 5, of which 3 were waited for; matrix products, arithmetic and copies ran while one was open for 29% of the time, Pallas kernels for 0%

commit v1 on v0

v1 whole, which is shorter than its diff:
```python
import functools

import jax
import jax.numpy as jnp
from jax import lax
from jax.experimental import pallas as pl
from jax.experimental.pallas import tpu as pltpu
from jax.sharding import PartitionSpec as P

MESH = pl.DeviceIdType.MESH
CHUNK = 128
NB = 512
F32 = jnp.float32
BF16 = jnp.bfloat16


def silu(v):
    return v * jax.nn.sigmoid(v)


def ssd_kernel(z_ref, x_ref, bc_ref, r_ref, prm_ref, bcp_ref, hp_ref, q_ref, xs, bs, state, qs, prev):
    chunk = pl.program_id(1)
    T = CHUNK
    width = xs.shape[1]

    @pl.when(chunk == 0)
    def _():
        xs[0:8, :] = jnp.zeros((8, width), F32)
        bs[0:8, :] = jnp.zeros((8, bs.shape[1]), F32)
        state[...] = jnp.zeros_like(state)

    @pl.when(chunk > 0)
    def _():
        xs[0:8, :] = xs[T:T + 8, :]
        bs[0:8, :] = bs[T:T + 8, :]

    xs[8:8 + T, :] = x_ref[0].astype(F32)
    bs[8:8 + T, :] = bc_ref[0].astype(F32)

    conv_bc = bcp_ref[0, 4:5, :]
    for tap in range(4):
        conv_bc = conv_bc + bs[5 + tap:5 + tap + T, :] * bcp_ref[0, tap:tap + 1, :]
    bc_act = silu(conv_bc).astype(BF16)
    n_state = bc_act.shape[1] // 2
    b_mat, c_mat = bc_act[:, :n_state], bc_act[:, n_state:]
    scores = lax.dot_general(c_mat, b_mat, (((1,), (1,)), ((), ())), preferred_element_type=F32)
    b_t = jnp.transpose(b_mat.astype(F32)).astype(BF16)

    dt = jax.nn.softplus(r_ref[0].astype(F32) + hp_ref[0, 0:1, :])
    log_a = hp_ref[0, 1:2, :] * dt
    row = lax.broadcasted_iota(jnp.int32, (T, T), 0)
    col = lax.broadcasted_iota(jnp.int32, (T, T), 1)
    causal = row >= col
    cum = jnp.dot(causal.astype(F32), log_a, preferred_element_type=F32, precision=lax.Precision.HIGHEST)
    cum_t = jnp.transpose(cum)
    dt_t = jnp.transpose(dt)
    left = lax.broadcasted_iota(jnp.int32, (T, 128), 1) < 64
    prev[...] = jnp.dot(c_mat, state[...].astype(BF16), preferred_element_type=F32)
    sq = jnp.zeros((T, 128), F32)

    for pair in range(width // 128):
        lanes = slice(pair * 128, pair * 128 + 128)
        conv = prm_ref[4:5, lanes]
        for tap in range(4):
            conv = conv + xs[5 + tap:5 + tap + T, lanes] * prm_ref[tap:tap + 1, lanes]
        u = silu(conv).astype(BF16)
        u32 = u.astype(F32)
        parts, cums, dts = [], [], []
        for half in range(2):
            h = 2 * pair + half
            cum_b = jnp.broadcast_to(cum[:, h:h + 1], (T, 128))
            decay = jnp.exp(jnp.where(causal, cum_b - cum_t[h:h + 1, :], -1e30))
            w = scores * decay * dt_t[h:h + 1, :]
            parts.append(jnp.dot(w.astype(BF16), u, preferred_element_type=F32))
            cums.append(cum_b)
            dts.append(jnp.broadcast_to(dt[:, h:h + 1], (T, 128)))
        cum_p = jnp.where(left, cums[0], cums[1])
        dt_p = jnp.where(left, dts[0], dts[1])
        end = cum_p[T - 1:T, :]
        y = jnp.where(left, parts[0], parts[1]) + jnp.exp(cum_p) * prev[:, lanes] + prm_ref[6:7, lanes] * u32
        xw = (u32 * (jnp.exp(end - cum_p) * dt_p)).astype(BF16)
        state[:, lanes] = jnp.exp(end) * state[:, lanes] + jnp.dot(b_t, xw, preferred_element_type=F32)
        gated = y * silu(z_ref[0, :, lanes].astype(F32))
        qs[:, lanes] = gated
        sq = sq + gated * gated

    inv = lax.rsqrt(jnp.sum(sq, axis=1, keepdims=True) / width + 1e-5)
    q_ref[...] = (qs[...] * inv * prm_ref[5:6, :]).astype(BF16)


def ssd_call(zx, bc, r, prm, bcp, hp):
    n_tok, inner = zx.shape[1], zx.shape[2]
    groups = bc.shape[0]
    width = inner // groups
    n_bc = bc.shape[2]
    T = CHUNK
    return pl.pallas_call(
        ssd_kernel,
        grid=(groups, n_tok // T),
        in_specs=[
            pl.BlockSpec((1, T, width), lambda g, c: (0, c, g)),
            pl.BlockSpec((1, T, width), lambda g, c: (1, c, g)),
            pl.BlockSpec((1, T, n_bc), lambda g, c: (g, c, 0)),
            pl.BlockSpec((1, T, 128), lambda g, c: (g, c, 0)),
            pl.BlockSpec((8, width), lambda g, c: (0, g)),
            pl.BlockSpec((1, 8, n_bc), lambda g, c: (g, 0, 0)),
            pl.BlockSpec((1, 8, 128), lambda g, c: (g, 0, 0)),
        ],
        out_specs=pl.BlockSpec((T, width), lambda g, c: (c, g)),
        out_shape=jax.ShapeDtypeStruct((n_tok, inner), BF16),
        scratch_shapes=[
            pltpu.VMEM((T + 8, width), F32),
            pltpu.VMEM((T + 8, n_bc), F32),
            pltpu.VMEM((n_bc // 2, width), F32),
            pltpu.VMEM((T, width), F32),
            pltpu.VMEM((T, width), F32),
        ],
        compiler_params=pltpu.CompilerParams(dimension_semantics=('arbitrary', 'arbitrary'), vmem_limit_bytes=48 * 2**20),
        cost_estimate=pl.CostEstimate(flops=8 * 10**9, bytes_accessed=14 * 2**20, transcendentals=10**7),
        name='ssd',
    )(zx, zx, bc, r, prm, bcp, hp)


def out_kernel(n_blk, rows, q_hbm, res_ref, w_ref, out_ref, qp, snd, own, rxs, rxx, ysnd, yrx, qsem, ss, rs, xs, xr, ys, yr):
    p, n = pl.program_id(0), pl.program_id(1)
    dp, sp, tp = lax.axis_index('dp'), lax.axis_index('sp'), lax.axis_index('tp')
    core = lax.rem(tp, 2)
    sib = tp + 1 - 2 * core
    across = lax.rem(tp + 2, 4)
    diag = lax.rem(sib + 2, 4)
    to_sib, to_x, to_y = (dp, sp, sib), (dp, sp, across), (dp, 1 - sp, tp)

    def q_copies(which):
        out = []
        for slot, quarter in enumerate(((diag, across), (sib, tp))[which]):
            for blk in range(2):
                src = q_hbm.at[pl.ds(pl.multiple_of(blk * 4 * rows + quarter * rows, rows), rows)]
                dst = qp.at[which, pl.ds((slot * 2 + blk) * rows, rows)]
                out.append(pltpu.make_async_copy(src, dst, qsem.at[which * 4 + slot * 2 + blk]))
        return out

    def sib_copy(k, m):
        return pltpu.make_async_remote_copy(
            src_ref=snd.at[k, m], dst_ref=rxs.at[k, m], send_sem=ss.at[k, m], recv_sem=rs.at[k, m],
            device_id=to_sib, device_id_type=MESH)

    def x_copy(m):
        return pltpu.make_async_remote_copy(
            src_ref=own.at[0, m], dst_ref=rxx.at[m], send_sem=xs.at[m], recv_sem=xr.at[m],
            device_id=to_x, device_id_type=MESH)

    def y_copy(m):
        return pltpu.make_async_remote_copy(
            src_ref=ysnd.at[m], dst_ref=yrx.at[m], send_sem=ys.at[m], recv_sem=yr.at[m],
            device_id=to_y, device_id_type=MESH)

    @pl.when(jnp.logical_and(p == 0, n == 0))
    def _():
        for copy in q_copies(0) + q_copies(1):
            copy.start()
        barrier = pltpu.get_barrier_semaphore()
        for peer in (to_sib, to_x, to_y):
            pl.semaphore_signal(barrier, inc=1, device_id=peer, device_id_type=MESH)
        pl.semaphore_wait(barrier, 3)
        for copy in q_copies(0) + q_copies(1):
            copy.wait()

    acc = jnp.dot(qp[p], w_ref[...], preferred_element_type=F32)
    snd[p, n] = acc[:2 * rows]
    own[p, n] = acc[2 * rows:]
    sib_copy(p, n).start()

    def forward(m):
        sib_copy(0, m).wait_recv()
        own[0, m] = own[0, m] + rxs[0, m]
        x_copy(m).start()

    @pl.when(jnp.logical_and(p == 0, n >= 1))
    def _():
        forward(n - 1)

    @pl.when(jnp.logical_and(p == 1, n == 0))
    def _():
        forward(n_blk - 1)

    @pl.when(jnp.logical_and(p == 1, n == n_blk - 1))
    def _():
        def finish(m, carry):
            sib_copy(1, m).wait_recv()
            x_copy(m).wait_recv()
            cols = pl.ds(pl.multiple_of(m * NB, NB), NB)
            for half, blk in enumerate((sp, 1 - sp)):
                part = pl.ds(pl.multiple_of(blk * rows, rows), rows)
                total = own[1, m, part] + rxs[1, m, part] + rxx[m, part] + res_ref[part, cols].astype(F32)
                if half == 0:
                    out_ref[sp, :, cols] = total.astype(BF16)
                else:
                    ysnd[m] = total.astype(BF16)
            y_copy(m).start()
            return carry

        lax.fori_loop(0, n_blk, finish, 0)

        def drain(m, carry):
            y_copy(m).wait_recv()
            cols = pl.ds(pl.multiple_of(m * NB, NB), NB)
            out_ref[1 - sp, :, cols] = yrx[m]
            sib_copy(0, m).wait_send()
            sib_copy(1, m).wait_send()
            x_copy(m).wait_send()
            y_copy(m).wait_send()
            return carry

        lax.fori_loop(0, n_blk, drain, 0)


def out_call(q, res, w_out):
    depth, d_model = w_out.shape
    rows = res.shape[0] // 2
    n_blk = d_model // NB
    blk2 = (2, n_blk, 2 * rows, NB)
    return pl.pallas_call(
        functools.partial(out_kernel, n_blk, rows),
        grid=(2, n_blk),
        in_specs=[
            pl.BlockSpec(memory_space=pl.ANY),
            pl.BlockSpec(memory_space=pltpu.VMEM),
            pl.BlockSpec((depth, NB), lambda p, n: (0, n)),
        ],
        out_specs=pl.BlockSpec(memory_space=pltpu.VMEM),
        out_shape=jax.ShapeDtypeStruct((2, rows, d_model), BF16),
        scratch_shapes=[
            pltpu.VMEM((2, 4 * rows, depth), BF16),
            pltpu.VMEM(blk2, F32),
            pltpu.VMEM(blk2, F32),
            pltpu.VMEM(blk2, F32),
            pltpu.VMEM(blk2[1:], F32),
            pltpu.VMEM((n_blk, rows, NB), BF16),
            pltpu.VMEM((n_blk, rows, NB), BF16),
            pltpu.SemaphoreType.DMA((8,)),
            pltpu.SemaphoreType.DMA((2, n_blk)),
            pltpu.SemaphoreType.DMA((2, n_blk)),
            pltpu.SemaphoreType.DMA((n_blk,)),
            pltpu.SemaphoreType.DMA((n_blk,)),
            pltpu.SemaphoreType.DMA((n_blk,)),
            pltpu.SemaphoreType.DMA((n_blk,)),
        ],
        compiler_params=pltpu.CompilerParams(
            dimension_semantics=('arbitrary', 'arbitrary'), collective_id=1, has_side_effects=True, vmem_limit_bytes=60 * 2**20),
        cost_estimate=pl.CostEstimate(flops=35 * 10**9, bytes_accessed=140 * 2**20, transcendentals=0),
        name='out_proj',
    )(q, res, w_out)


def solution(mesh):
    tp_size = mesh.shape['tp']
    tok_spec = P('dp', ('sp', 'tp'), None)

    def local_layer(x_loc, w_zx, w_dt, w_bc, conv_x, conv_bc, bias_x, bias_bc, a_log, dt_bias, d_skip, norm_w, w_out):
        rows, d_model = x_loc.shape[1], x_loc.shape[2]
        groups = w_bc.shape[2]
        heads = a_log.shape[0]
        inner = w_zx.shape[2]
        g_loc = groups // tp_size
        per_group = heads // g_loc
        sp, tp = lax.axis_index('sp'), lax.axis_index('tp')
        first = tp * g_loc
        w_bc_loc = lax.dynamic_slice_in_dim(w_bc, first, g_loc, axis=2)
        conv_bc_loc = lax.dynamic_slice_in_dim(conv_bc, first, g_loc, axis=2)
        bias_bc_loc = lax.dynamic_slice_in_dim(bias_bc, first, g_loc, axis=1)

        mine = jnp.where(sp == 0, x_loc[0], x_loc[1])
        other = jnp.where(sp == 0, x_loc[1], x_loc[0])
        got = lax.ppermute(other, 'sp', [(0, 1), (1, 0)])
        x_pair = jnp.stack([jnp.where(sp == 0, mine, got), jnp.where(sp == 0, got, mine)])
        x_all = lax.all_gather(x_pair, 'tp', axis=1, tiled=True).reshape(-1, d_model)

        n_tok = x_all.shape[0]
        n_state = w_bc.shape[3]
        bc = jnp.einsum('md,dcgn->gmcn', x_all, w_bc_loc, preferred_element_type=F32).astype(BF16)
        bc = bc.reshape(g_loc, n_tok, 2 * n_state)
        r = jnp.einsum('md,dh->mh', x_all, w_dt, preferred_element_type=F32).astype(BF16)
        r = jnp.moveaxis(r.reshape(n_tok, g_loc, per_group), 1, 0)
        r = jnp.pad(r, ((0, 0), (0, 0), (0, 128 - per_group)))
        zx = jnp.einsum('md,dcn->cmn', x_all, w_zx, preferred_element_type=F32).astype(BF16)

        skip = jnp.repeat(d_skip, inner // heads)
        prm = jnp.concatenate([conv_x.astype(F32), bias_x.astype(F32)[None], norm_w.astype(F32)[None], skip[None], jnp.zeros((1, inner), F32)])
        taps = jnp.moveaxis(conv_bc_loc.astype(F32), 2, 0).reshape(g_loc, 4, 2 * n_state)
        bias = jnp.moveaxis(bias_bc_loc.astype(F32), 1, 0).reshape(g_loc, 1, 2 * n_state)
        bcp = jnp.concatenate([taps, bias, jnp.zeros((g_loc, 3, 2 * n_state), F32)], axis=1)
        hp = jnp.stack([dt_bias, -jnp.exp(a_log)]).reshape(2, g_loc, per_group)
        hp = jnp.pad(jnp.moveaxis(hp, 1, 0), ((0, 0), (0, 6), (0, 128 - per_group)))

        q = ssd_call(zx, bc, r, prm, bcp, hp)
        return out_call(q, x_pair.reshape(2 * rows, d_model), w_out)

    in_specs = (tok_spec, P(None, None, 'tp'), P(None, 'tp'), P(), P(None, 'tp'), P(), P('tp'), P(), P('tp'), P('tp'), P('tp'), P('tp'), P('tp', None))
    return jax.shard_map(local_layer, mesh=mesh, in_specs=in_specs, out_specs=tok_spec, check_vma=False)
```

time: 517 us -> 356 us (0.69); the launches traced: 509 us -> 355 us
  waiting for transfers between devices: 214 us -> 50.9 us
  Pallas kernels: 0 us -> 136 us
  matrix products: 185 us -> 109 us
  other arithmetic: 46.7 us -> 6.57 us
  local copies, waits for them, and re-layouts: 40.6 us -> 34.6 us
  starting transfers between devices: 8.96 us -> 3.43 us
    pallas_call x0 -> x2, Pallas kernels: none -> 136 us  [the longest x1 106 us: out_call(): pl.pallas_call(functools.partial(out_kernel, n_blk, rows), grid=(2, n_blk...]
    reduce_scatter x1 -> x0, waiting for transfers between devices: 120 us -> none  [local_layer(): out_loc = lax.psum_scatter(out_part, 'tp', scatter_dimension=1, tiled=True)]
    dot_general x9 -> x3, matrix products: 185 us -> 109 us  [the longest x1 88.5 us: local_layer(): jnp.einsum('md,dcn->cmn', x_all, w_zx, preferred_element_type=F32)]
    ppermute x3 -> x1, waiting for transfers between devices: 66.9 us -> 23.2 us  [local_layer(): got = lax.ppermute(other, 'sp', [(0, 1), (1, 0)])]
    convert_element_type x10 -> x0, other arithmetic: 38.8 us -> none  [the longest x2 16.9 us: causal_conv(): return jax.nn.silu(conv_sum).astype(jnp.bfloat16)]
    ppermute x3 -> x1, starting transfers between devices: 8.92 us -> 3.39 us  [local_layer(): got = lax.ppermute(other, 'sp', [(0, 1), (1, 0)])]
  transfers between devices with their start and end apart: 5 -> 2, of which waited for: 3 -> 2; matrix products, arithmetic and copies ran while one was open for 29% -> 8% of each run, Pallas kernels for 0% -> 0%
where the time goes in v1:
time: 356 us; the launch traced here: 355 us
  Pallas kernels  136 us (38%)
  matrix products  109 us (31%)
  waiting for transfers between devices  50.9 us (14%)
  local copies, waits for them, and re-layouts  34.6 us (10%)
  between operations  13.6 us (4%)
  other arithmetic  6.57 us (2%)
    pallas_call x1, Pallas kernels, out_call(): pl.pallas_call(functools.partial(out_kernel, n_blk, rows), grid=(2, n_blk...  106 us
    dot_general x1, matrix products, local_layer(): jnp.einsum('md,dcn->cmn', x_all, w_zx, preferred_element_type=F32)  88.5 us
    pallas_call x1, Pallas kernels, ssd_call(): pl.pallas_call(ssd_kernel, grid=(groups, n_tok // T), in_specs=[pl.BlockS...  30.2 us
    all_gather x1, waiting for transfers between devices, local_layer(): lax.all_gather(x_pair, 'tp', axis=1, tiled=True).reshape(-1, d_model)  27.7 us
    dynamic_slice x1, local copies, waits for them, and re-layouts, local_layer(): w_bc_loc = lax.dynamic_slice_in_dim(w_bc, first, g_loc, axis=2)  27.1 us
    ppermute x1, waiting for transfers between devices, local_layer(): got = lax.ppermute(other, 'sp', [(0, 1), (1, 0)])  23.2 us
    dot_general x1, matrix products, local_layer(): jnp.einsum('md,dcgn->gmcn', x_all, w_bc_loc, preferred_element_type=F32)  14.9 us
  transfers between devices with their start and end apart: 2, of which 2 were waited for; matrix products, arithmetic and copies ran while one was open for 8% of the time, Pallas kernels for 0%

profile of v1, /device:TPU:0, one launch (start us, length us, event | category | flops | bytes accessed | tf_op | source)
XLA Modules:
  0.0 354.5 jit_solution(11208106309888824500)
XLA Ops:
  6.5 0.0 copy-start
  6.5 0.0 copy-start.7
  6.6 0.0 copy-start.2
  6.6 0.0 all-gather.2.cloned.1.call-start
  6.6 1.7 select_bitcast_fusion
  8.4 3.4 collective-permute-start
  11.8 23.2 %collective-permute-done = bf16[64,8192]{1,0:T(8,128)(2,1)S(1)} collective-permute-done((bf16[64,8192]{1,0:T(8,128)(2,1)S(1)}, bf16[64,8192]{1,0:T(8,128)(2,1)S(1)}, u32[]{:S(2)}, u32[]{:S(2)}) %collective-permute-start) | collective-permute-done | bytes 1048608 | tf_op jit(solution)/shard_map/ppermute | solution.py:274
  34.9 1.7 fusion.12
  36.7 1.5 pad_maximum_fusion
  38.2 0.0 all-gather.2.cloned.1.call-update
  38.2 0.8 convert_bitcast_fusion.1
  39.0 0.7 convert_bitcast_fusion.2
  39.8 0.1 broadcast_in_dim.25
  39.8 0.1 broadcast_in_dim_reshape.3
  40.0 0.1 stack.22
  40.1 0.1 stack.21
  40.2 0.1 pad.14.clone
  40.3 0.1 concatenate.7.prm_ref
  40.4 0.1 maximum_maximum_fusion.bcp_ref
  40.5 27.1 %constant_dynamic-slice_fusion = bf16[8192,2,2,256]{3,2,1,0:T(2,128)(2,1)} fusion(bf16[8192,2,8,256]{3,2,1,0:T(8,128)(2,1)} %param.16, s32[]{:T(128)S(6)} %select_n.41), kind=kLoop, calls=%fused_computation.19 | loop fusion | bytes 33554436 | tf_op jit(solution)/shard_map/dynamic_slice | solution.py:268
  67.6 27.7 %all-gather.2.cloned.1.call-done = bf16[2,256,8192]{2,1,0:T(8,128)(2,1)} async-done(((bf16[2,64,8192]{2,1,0:T(8,128)(2,1)}), bf16[2,256,8192]{2,1,0:T(8,128)(2,1)}) %all-gather.2.cloned.1.call-update) | async-done | bytes 8388624 | tf_op jit(solution)/shard_map/all_gather | solution.py:276
  95.3 14.9 %fusion.9 = bf16[2,512,2,256]{1,3,0,2:T(8,128)(2,1)S(1)} fusion(bf16[512,8192,1,1]{1,0,3,2:T(8,128)(2,1)} %bitcast.41, bf16[8192,2,2,256]{3,2,1,0:T(2,128)(2,1)} %constant_dynamic-slice_fusion), kind=kOutput, calls=%fused_computation.7 | convolution fusion | flops 8590458880 | bytes 26214400 | tf_op jit(solution)/shard_map/md,dcgn->gmcn/dot_general | solution.py:280
  110.2 0.9 copy.23
  111.1 0.7 reshape.34.bc_ref
  111.8 6.0 %convolution_convert_fusion = bf16[512,64]{0,1:T(8,128)(2,1)S(1)} fusion(bf16[512,8192]{1,0:T(8,128)(2,1)} %bitcast.42, bf16[8192,64]{0,1:T(8,128)(2,1)S(1)} %copy-done), kind=kOutput, calls=%fused_computation.8 | convolution fusion | flops 536903680 | bytes 9502720 | tf_op jit(solution)/shard_map/md,dh->mh/dot_general | solution.py:282
  117.8 0.2 copy.24
  118.0 88.5 %convert_bitcast_fusion.z_ref.x_ref = bf16[2,512,4096]{2,1,0:T(8,128)(2,1)} fusion(bf16[512,8192,1]{1,0,2:T(8,128)(2,1)} %bitcast.43, bf16[8192,2,4096]{2,1,0:T(2,128)(2,1)} %param.14), kind=kOutput, calls=%fused_computation.4 | convolution fusion | flops 68723671040 | bytes 150994944 | tf_op jit(solution)/shard_map/md,dcn->cmn/dot_general | solution.py:285
  206.5 0.1 pad.8.r_ref
  206.6 30.2 %ssd.1.q_hbm = bf16[512,4096]{1,0:T(8,128)(2,1)S(1)} custom-call(bf16[2,512,4096]{2,1,0:T(8,128)(2,1)} %convert_bitcast_fusion.z_ref.x_ref, bf16[2,512,4096]{2,1,0:T(8,128)(2,1)} %convert_bitcast_fusion.z_ref.x_ref, bf16[2,512,512]{2,1,0:T(8,128)(2,1)S(1)} %reshape.34.bc_ref, bf16[2,512,128]{2,1,0:T(8,128)(2,1)S(1)} %pad.8.r_ref, ...), custom_call_target="tpu_custom_call" | custom-call | flops 8000000000 | bytes 14680064 | tf_op jit(solution)/shard_map/ssd/pallas_call | solution.py:97
  236.8 1.9 copy-done.1
  238.7 105.8 %out_proj.1 = bf16[2,64,8192]{2,1,0:T(8,128)(2,1)} custom-call(bf16[512,4096]{1,0:T(8,128)(2,1)} %copy-done.1, bf16[128,8192]{1,0:T(8,128)(2,1)} %bitcast.44, bf16[4096,8192]{1,0:T(8,128)(2,1)} %w_ref.1), custom_call_target="tpu_custom_call" | custom-call | flops 35000000512 | bytes 146800640 | tf_op jit(solution)/shard_map/out_proj/pallas_call | solution.py:222
  344.6 3.1 copy.42
  (23 shorter events, 0.1 us)
Async XLA Ops:
  6.5 105.2 %copy-start = (bf16[8192,64]{0,1:T(8,128)(2,1)S(1)}, bf16[8192,64]{0,1:T(8,128)(2,1)}, u32[]{:S(2)}) copy-start(bf16[8192,64]{0,1:T(8,128)(2,1)} %param.15) | copy-start | bytes 3145732
  6.5 33.2 %copy-start.5 = (f32[64]{0:T(128)S(1)}, f32[64]{0:T(128)}, u32[]{:S(2)}) copy-start(f32[64]{0:T(128)} %param.23) | copy-start | bytes 772
  6.5 33.4 %copy-start.3 = (bf16[4096]{0:T(1024)(128)(2,1)S(1)}, bf16[4096]{0:T(1024)(128)(2,1)}, u32[]{:S(2)}) copy-start(bf16[4096]{0:T(1024)(128)(2,1)} %param.19) | copy-start | bytes 24580
  6.5 33.4 %copy-start.4 = (bf16[4096]{0:T(1024)(128)(2,1)S(1)}, bf16[4096]{0:T(1024)(128)(2,1)}, u32[]{:S(2)}) copy-start(bf16[4096]{0:T(1024)(128)(2,1)} %param.24) | copy-start | bytes 24580
  6.5 33.4 %copy-start.6 = (f32[64]{0:T(128)S(1)}, f32[64]{0:T(128)}, u32[]{:S(2)}) copy-start(f32[64]{0:T(128)} %param.21) | copy-start | bytes 772
  6.5 33.5 %copy-start.7 = (f32[64]{0:T(128)S(1)}, f32[64]{0:T(128)}, u32[]{:S(2)}) copy-start(f32[64]{0:T(128)} %param.22) | copy-start | bytes 772
  6.6 33.7 %copy-start.2 = (bf16[4,4096]{1,0:T(4,128)(2,1)S(1)}, bf16[4,4096]{1,0:T(4,128)(2,1)}, u32[]{:S(2)}) copy-start(bf16[4,4096]{1,0:T(4,128)(2,1)} %param.17) | copy-start | bytes 98308
  6.6 88.7 %all-gather.2.cloned.1.call-start = ((), (), s32[]{:S(2)}) async-start(), calls=%async_computation | async-start | bytes 10485760 | tf_op jit(solution)/shard_map/all_gather | solution.py:276
  8.4 26.5 %collective-permute-start = (bf16[64,8192]{1,0:T(8,128)(2,1)S(1)}, bf16[64,8192]{1,0:T(8,128)(2,1)S(1)}, u32[]{:S(2)}, u32[]{:S(2)}) collective-permute-start(bf16[64,8192]{1,0:T(8,128)(2,1)S(1)} %select_bitcast_fusion), channel_id=1, source_target_pairs={{0,4},{4,0},{1,5},{5,1},{2,6},{6,2},{3,7},{7,3}} | collective-permute-start | bytes 3145736 | tf_op jit(solution)/shard_map/ppermute | solution.py:274
  236.8 2.0 copy-start.1
Sparse Core Ops, SparseCore 0:
  38.3 56.9 all-gather.1

commit v2 on v1

--- a/solution.py
+++ b/solution.py
@@ -121,7 +121,7 @@
     )(zx, zx, bc, r, prm, bcp, hp)
 
 
-def out_kernel(n_blk, rows, q_hbm, res_ref, w_ref, out_ref, qp, snd, own, rxs, rxx, ysnd, yrx, qsem, ss, rs, xs, xr, ys, yr):
+def out_kernel(n_blk, rows, q_hbm, x_hbm, w_ref, out_ref, res_ref, qp, snd, own, rxs, rxx, ysnd, yrx, qsem, ss, rs, xs, xr, ys, yr):
     p, n = pl.program_id(0), pl.program_id(1)
     dp, sp, tp = lax.axis_index('dp'), lax.axis_index('sp'), lax.axis_index('tp')
     core = lax.rem(tp, 2)
@@ -139,6 +139,11 @@
                 out.append(pltpu.make_async_copy(src, dst, qsem.at[which * 4 + slot * 2 + blk]))
         return out
 
+    def res_copies():
+        return [pltpu.make_async_copy(
+            x_hbm.at[pl.ds(pl.multiple_of(blk * 4 * rows + tp * rows, rows), rows)],
+            res_ref.at[pl.ds(blk * rows, rows)], qsem.at[8 + blk]) for blk in range(2)]
+
     def sib_copy(k, m):
         return pltpu.make_async_remote_copy(
             src_ref=snd.at[k, m], dst_ref=rxs.at[k, m], send_sem=ss.at[k, m], recv_sem=rs.at[k, m],
@@ -156,13 +161,13 @@
 
     @pl.when(jnp.logical_and(p == 0, n == 0))
     def _():
-        for copy in q_copies(0) + q_copies(1):
+        for copy in q_copies(0) + q_copies(1) + res_copies():
             copy.start()
         barrier = pltpu.get_barrier_semaphore()
         for peer in (to_sib, to_x, to_y):
             pl.semaphore_signal(barrier, inc=1, device_id=peer, device_id_type=MESH)
         pl.semaphore_wait(barrier, 3)
-        for copy in q_copies(0) + q_copies(1):
+        for copy in q_copies(0) + q_copies(1) + res_copies():
             copy.wait()
 
     acc = jnp.dot(qp[p], w_ref[...], preferred_element_type=F32)
@@ -214,9 +219,8 @@
         lax.fori_loop(0, n_blk, drain, 0)
 
 
-def out_call(q, res, w_out):
+def out_call(q, x_all, w_out, rows):
     depth, d_model = w_out.shape
-    rows = res.shape[0] // 2
     n_blk = d_model // NB
     blk2 = (2, n_blk, 2 * rows, NB)
     return pl.pallas_call(
@@ -224,12 +228,13 @@
         grid=(2, n_blk),
         in_specs=[
             pl.BlockSpec(memory_space=pl.ANY),
-            pl.BlockSpec(memory_space=pltpu.VMEM),
+            pl.BlockSpec(memory_space=pl.ANY),
             pl.BlockSpec((depth, NB), lambda p, n: (0, n)),
         ],
         out_specs=pl.BlockSpec(memory_space=pltpu.VMEM),
         out_shape=jax.ShapeDtypeStruct((2, rows, d_model), BF16),
         scratch_shapes=[
+            pltpu.VMEM((2 * rows, d_model), BF16),
             pltpu.VMEM((2, 4 * rows, depth), BF16),
             pltpu.VMEM(blk2, F32),
             pltpu.VMEM(blk2, F32),
@@ -237,7 +242,7 @@
             pltpu.VMEM(blk2[1:], F32),
             pltpu.VMEM((n_blk, rows, NB), BF16),
             pltpu.VMEM((n_blk, rows, NB), BF16),
-            pltpu.SemaphoreType.DMA((8,)),
+            pltpu.SemaphoreType.DMA((10,)),
             pltpu.SemaphoreType.DMA((2, n_blk)),
             pltpu.SemaphoreType.DMA((2, n_blk)),
             pltpu.SemaphoreType.DMA((n_blk,)),
@@ -249,7 +254,168 @@
             dimension_semantics=('arbitrary', 'arbitrary'), collective_id=1, has_side_effects=True, vmem_limit_bytes=60 * 2**20),
         cost_estimate=pl.CostEstimate(flops=35 * 10**9, bytes_accessed=140 * 2**20, transcendentals=0),
         name='out_proj',
-    )(q, res, w_out)
+    )(q, x_all, w_out)
+
+
+def gather_kernel(n_chunk, x_hbm, w_ref, wdt_ref, xall_ref, bc_ref, r_ref, xg, wv, acc, racc, lsem, wsem, osem, ss, rs):
+    dp, sp, tp = lax.axis_index('dp'), lax.axis_index('sp'), lax.axis_index('tp')
+    rows = x_hbm.shape[1]
+    width = xg.shape[2]
+    half = width // 2
+    core = lax.rem(tp, 2)
+    sib = tp + 1 - 2 * core
+    across = lax.rem(tp + 2, 4)
+    diag = lax.rem(sib + 2, 4)
+    to_sib, to_x, to_y = (dp, sp, sib), (dp, sp, across), (dp, 1 - sp, tp)
+
+    def slot(k, blk, owner):
+        return xg.at[k, pl.ds(pl.multiple_of((blk * 4 + owner) * rows, rows), rows)]
+
+    def columns(seq, k):
+        return x_hbm.at[seq, :, pl.ds(k * width, width)]
+
+    def local(k):
+        return pltpu.make_async_copy(columns(sp, k), slot(k, sp, tp), lsem.at[k])
+
+    def weights(k):
+        return [pltpu.make_async_copy(
+            w_ref.at[pl.ds(k * half, half), par, c, j, tp], wv.at[k, par, c, j], wsem.at[k, par * 4 + c * 2 + j])
+            for par in range(2) for c in range(2) for j in range(2)]
+
+    def send(kind, k):
+        source, target = [
+            (None, to_y),
+            ((sp, tp), to_x), ((1 - sp, tp), to_x),
+            ((sp, tp), to_sib), ((1 - sp, tp), to_sib),
+            ((sp, across), to_sib), ((1 - sp, across), to_sib),
+        ][kind]
+        if source is None:
+            src, dst = columns(1 - sp, k), slot(k, sp, tp)
+        else:
+            src = dst = slot(k, *source)
+        return pltpu.make_async_remote_copy(
+            src_ref=src, dst_ref=dst, send_sem=ss.at[kind, k], recv_sem=rs.at[kind, k],
+            device_id=target, device_id_type=MESH)
+
+    def arrived(kind, k):
+        blk, owner = [(1 - sp, tp), (sp, across), (1 - sp, across), (sp, sib), (1 - sp, sib), (sp, diag), (1 - sp, diag)][kind]
+        here = slot(k, blk, owner)
+        pltpu.make_async_remote_copy(
+            src_ref=here, dst_ref=here, send_sem=ss.at[kind, k], recv_sem=rs.at[kind, k],
+            device_id=to_sib, device_id_type=MESH).wait_recv()
+
+    def store(k):
+        return pltpu.make_async_copy(xg.at[k], xall_ref.at[:, pl.ds(k * width, width)], osem.at[k])
+
+    for k in range(n_chunk):
+        local(k).start()
+    for k in range(n_chunk):
+        for copy in weights(k):
+            copy.start()
+    barrier = pltpu.get_barrier_semaphore()
+    for peer in (to_sib, to_x, to_y):
+        pl.semaphore_signal(barrier, inc=1, device_id=peer, device_id_type=MESH)
+    pl.semaphore_wait(barrier, 3)
+
+    def own_out(k):
+        local(k).wait()
+        send(1, k).start()
+        send(3, k).start()
+
+    def swapped_out(k):
+        arrived(0, k)
+        send(2, k).start()
+        send(4, k).start()
+
+    step = 512
+    even = lax.rem(lax.broadcasted_iota(jnp.int32, (step // 8, 8, 128), 1), 2) == 0
+
+    def compute(k):
+        arrived(1, k)
+        send(5, k).start()
+        arrived(2, k)
+        send(6, k).start()
+        for copy in weights(k):
+            copy.wait()
+        for kind in range(3, 7):
+            arrived(kind, k)
+        store(k).start()
+
+        def part(i, carry):
+            span = pl.ds(pl.multiple_of(i * step, step), step)
+            lhs = xg[k, :, span]
+            for c in range(2):
+                first, second = [], []
+                for j in range(2):
+                    a = wv.at[k, 0, c, j].reshape(width, 128)[span, :].astype(F32).reshape(step // 8, 8, 128)
+                    b = wv.at[k, 1, c, j].reshape(width, 128)[span, :].astype(F32).reshape(step // 8, 8, 128)
+                    first.append(jnp.where(even, a, pltpu.roll(b, 1, 1)).reshape(step, 128).astype(BF16))
+                    second.append(jnp.where(even, pltpu.roll(a, 7, 1), b).reshape(step, 128).astype(BF16))
+                for g, pieces in enumerate((first, second)):
+                    acc[g, c] += jnp.dot(lhs, jnp.concatenate(pieces, axis=1), preferred_element_type=F32)
+            return carry
+
+        lax.fori_loop(0, width // step, part, 0)
+        racc[...] += lax.dot_general(
+            xg[k], wdt_ref[:, k * width:(k + 1) * width], (((1,), (1,)), ((), ())), preferred_element_type=F32)
+
+    for k in range(n_chunk):
+        send(0, k).start()
+    acc[...] = jnp.zeros_like(acc)
+    racc[...] = jnp.zeros_like(racc)
+    own_out(0)
+    own_out(1)
+    swapped_out(0)
+    own_out(2)
+    swapped_out(1)
+    own_out(3)
+    compute(0)
+    swapped_out(2)
+    compute(1)
+    swapped_out(3)
+    compute(2)
+    compute(3)
+
+    for g in range(2):
+        for c in range(2):
+            bc_ref[g, :, c * 256:(c + 1) * 256] = acc[g, c].astype(BF16)
+    r_ref[...] = racc[...].astype(BF16)
+    for k in range(n_chunk):
+        for kind in range(7):
+            send(kind, k).wait_send()
+        store(k).wait()
+
+
+def gather_call(x_loc, w_bc, w_dt):
+    n_seq, rows, d_model = x_loc.shape
+    n_tok = 8 * rows
+    n_chunk = 4
+    width = d_model // n_chunk
+    heads = w_dt.shape[1]
+    w_view = w_bc.reshape(d_model // 2, 2, 2, 4, 2, 2, 128).transpose(0, 1, 2, 5, 3, 4, 6)
+    anywhere = pl.BlockSpec(memory_space=pl.ANY)
+    vmem = pl.BlockSpec(memory_space=pltpu.VMEM)
+    dma = pltpu.SemaphoreType.DMA
+    return pl.pallas_call(
+        functools.partial(gather_kernel, n_chunk),
+        in_specs=[anywhere, anywhere, vmem],
+        out_specs=(anywhere, vmem, vmem),
+        out_shape=(
+            jax.ShapeDtypeStruct((n_tok, d_model), BF16),
+            jax.ShapeDtypeStruct((2, n_tok, 512), BF16),
+            jax.ShapeDtypeStruct((n_tok, heads), BF16),
+        ),
+        scratch_shapes=[
+            pltpu.VMEM((n_chunk, n_tok, width), BF16),
+            pltpu.VMEM((n_chunk, 2, 2, 2, width // 2, 2, 128), BF16),
+            pltpu.VMEM((2, 2, n_tok, 256), F32),
+            pltpu.VMEM((n_tok, heads), F32),
+            dma((n_chunk,)), dma((n_chunk, 8)), dma((n_chunk,)), dma((7, n_chunk)), dma((7, n_chunk)),
+        ],
+        compiler_params=pltpu.CompilerParams(collective_id=2, has_side_effects=True, vmem_limit_bytes=48 * 2**20),
+        cost_estimate=pl.CostEstimate(flops=10**10, bytes_accessed=30 * 2**20, transcendentals=0),
+        name='gather_bc',
+    )(x_loc, w_view, w_dt.T)
 
 
 def solution(mesh):
@@ -265,21 +431,12 @@
         per_group = heads // g_loc
         sp, tp = lax.axis_index('sp'), lax.axis_index('tp')
         first = tp * g_loc
-        w_bc_loc = lax.dynamic_slice_in_dim(w_bc, first, g_loc, axis=2)
         conv_bc_loc = lax.dynamic_slice_in_dim(conv_bc, first, g_loc, axis=2)
         bias_bc_loc = lax.dynamic_slice_in_dim(bias_bc, first, g_loc, axis=1)
 
-        mine = jnp.where(sp == 0, x_loc[0], x_loc[1])
-        other = jnp.where(sp == 0, x_loc[1], x_loc[0])
-        got = lax.ppermute(other, 'sp', [(0, 1), (1, 0)])
-        x_pair = jnp.stack([jnp.where(sp == 0, mine, got), jnp.where(sp == 0, got, mine)])
-        x_all = lax.all_gather(x_pair, 'tp', axis=1, tiled=True).reshape(-1, d_model)
-
+        x_all, bc, r = gather_call(x_loc, w_bc, w_dt)
         n_tok = x_all.shape[0]
         n_state = w_bc.shape[3]
-        bc = jnp.einsum('md,dcgn->gmcn', x_all, w_bc_loc, preferred_element_type=F32).astype(BF16)
-        bc = bc.reshape(g_loc, n_tok, 2 * n_state)
-        r = jnp.einsum('md,dh->mh', x_all, w_dt, preferred_element_type=F32).astype(BF16)
         r = jnp.moveaxis(r.reshape(n_tok, g_loc, per_group), 1, 0)
         r = jnp.pad(r, ((0, 0), (0, 0), (0, 128 - per_group)))
         zx = jnp.einsum('md,dcn->cmn', x_all, w_zx, preferred_element_type=F32).astype(BF16)
@@ -293,7 +450,7 @@
         hp = jnp.pad(jnp.moveaxis(hp, 1, 0), ((0, 0), (0, 6), (0, 128 - per_group)))
 
         q = ssd_call(zx, bc, r, prm, bcp, hp)
-        return out_call(q, x_pair.reshape(2 * rows, d_model), w_out)
+        return out_call(q, x_all, w_out, rows)
 
     in_specs = (tok_spec, P(None, None, 'tp'), P(None, 'tp'), P(), P(None, 'tp'), P(), P('tp'), P(), P('tp'), P('tp'), P('tp'), P('tp'), P('tp', None))
     return jax.shard_map(local_layer, mesh=mesh, in_specs=in_specs, out_specs=tok_spec, check_vma=False)

time: 356 us -> 301 us (0.85)
  Pallas kernels: 136 us -> 197 us
  waiting for transfers between devices: 50.9 us -> 0 us
  local copies, waits for them, and re-layouts: 34.6 us -> 10.8 us
  matrix products: 109 us -> 88.5 us
  between operations: 13.6 us -> 0.1 us
    pallas_call x0 -> x1, Pallas kernels: none -> 60.7 us  [gather_call(): pl.pallas_call(functools.partial(gather_kernel, n_chunk), in_specs=[anywh...]
    all_gather x1 -> x0, waiting for transfers between devices: 27.7 us -> none  [local_layer(): lax.all_gather(x_pair, 'tp', axis=1, tiled=True).reshape(-1, d_model)]
    dynamic_slice x1 -> x0, local copies, waits for them, and re-layouts: 27.1 us -> none  [local_layer(): w_bc_loc = lax.dynamic_slice_in_dim(w_bc, first, g_loc, axis=2)]
    ppermute x1 -> x0, waiting for transfers between devices: 23.2 us -> none  [local_layer(): got = lax.ppermute(other, 'sp', [(0, 1), (1, 0)])]
    dot_general x2 -> x0, matrix products: 20.9 us -> none  [the longest x1 14.9 us: local_layer(): jnp.einsum('md,dcgn->gmcn', x_all, w_bc_loc, preferred_element_type=F32)]
    unnamed x17 -> x7, local copies, waits for them, and re-layouts: 5.07 us -> 7.85 us
  transfers between devices with their start and end apart: 2 -> 0, of which waited for: 2 -> 0; matrix products, arithmetic and copies ran while one was open for 8% -> 0% of each run, Pallas kernels for 0% -> 0%
where the time goes in v2:
time: 301 us; the launch traced here: 300 us
  Pallas kernels  197 us (65%)
  matrix products  88.5 us (29%)
  local copies, waits for them, and re-layouts  10.8 us (4%)
  other arithmetic  3.62 us (1%)
    pallas_call x1, Pallas kernels, out_call(): pl.pallas_call(functools.partial(out_kernel, n_blk, rows), grid=(2, n_blk...  106 us
    dot_general x1, matrix products, local_layer(): jnp.einsum('md,dcn->cmn', x_all, w_zx, preferred_element_type=F32)  88.5 us
    pallas_call x1, Pallas kernels, gather_call(): pl.pallas_call(functools.partial(gather_kernel, n_chunk), in_specs=[anywh...  60.7 us
    pallas_call x1, Pallas kernels, ssd_call(): pl.pallas_call(ssd_kernel, grid=(groups, n_tok // T), in_specs=[pl.BlockS...  30.2 us
    unnamed x7, local copies, waits for them, and re-layouts  7.85 us

profile of v2, /device:TPU:0, one launch (start us, length us, event | category | flops | bytes accessed | tf_op | source)
XLA Modules:
  0.0 299.7 jit_solution(12706324118547545527)
XLA Ops:
  0.0 0.7 exponential_negate_fusion
  0.7 0.1 stack.10
  0.7 0.1 pad.14.clone
  0.8 0.7 stack.9
  1.6 0.7 convert_bitcast_fusion.2
  2.3 0.8 convert_bitcast_fusion.1
  3.1 0.1 maximum_maximum_fusion.bcp_ref
  3.2 0.7 broadcast_in_dim.28
  3.9 0.7 broadcast_in_dim.29
  4.6 0.7 broadcast_in_dim.25
  5.3 0.1 broadcast_in_dim_reshape.3
  5.4 0.9 concatenate.7.prm_ref
  6.3 0.0 copy-start
  6.3 1.6 copy-done
  7.9 0.0 copy-start.1
  7.9 1.2 copy-done.1
  9.1 60.7 %gather_bc.1 = (bf16[512,8192]{1,0:T(8,128)(2,1)}, bf16[2,512,512]{2,1,0:T(8,128)(2,1)S(1)}, bf16[512,64]{1,0:T(8,128)(2,1)S(1)}) custom-call(bf16[2,64,8192]{2,1,0:T(8,128)(2,1)S(1)} %copy-done, bf16[4096,2,2,2,4,2,128]{6,5,4,3,2,1,0:T(2,128)(2,1)} %bitcast.1.w_ref, bf16[64,8192]{1,0:T(8,128)(2,1)S(1)} %bitcast.23), custom_call_target="tpu_custom_call" | custom-call | flops 10000000000 | bytes 31457280 | tf_op jit(solution)/shard_map/gather_bc/pallas_call | solution.py:399
  69.8 0.1 copy.20
  69.9 0.2 copy.21
  70.1 0.1 pad.8.r_ref
  70.2 88.5 %convert_bitcast_fusion.z_ref.x_ref = bf16[2,512,4096]{2,1,0:T(8,128)(2,1)} fusion(bf16[8192,2,4096]{2,1,0:T(2,128)(2,1)} %param.14, bf16[512,8192]{1,0:T(8,128)(2,1)} %get-tuple-element.8.x_hbm), kind=kOutput, calls=%fused_computation.3 | convolution fusion | flops 68723671040 | bytes 150994944 | tf_op jit(solution)/shard_map/md,dcn->cmn/dot_general | solution.py:442
  158.6 30.2 %ssd.1.q_hbm = bf16[512,4096]{1,0:T(8,128)(2,1)S(1)} custom-call(bf16[2,512,4096]{2,1,0:T(8,128)(2,1)} %convert_bitcast_fusion.z_ref.x_ref, bf16[2,512,4096]{2,1,0:T(8,128)(2,1)} %convert_bitcast_fusion.z_ref.x_ref, bf16[2,512,512]{2,1,0:T(8,128)(2,1)S(1)} %get-tuple-element.9.bc_ref, bf16[2,512,128]{2,1,0:T(8,128)(2,1)S(1)} %pad.8.r_ref, ...), custom_call_target="tpu_custom_call" | custom-call | flops 8000000000 | bytes 14680064 | tf_op jit(solution)/shard_map/ssd/pallas_call | solution.py:97
  188.8 0.0 copy-start.2
  188.8 1.9 copy-done.2
  190.8 105.9 %out_proj.1 = bf16[2,64,8192]{2,1,0:T(8,128)(2,1)} custom-call(bf16[512,4096]{1,0:T(8,128)(2,1)} %copy-done.2, bf16[512,8192]{1,0:T(8,128)(2,1)} %get-tuple-element.8.x_hbm, bf16[4096,8192]{1,0:T(8,128)(2,1)} %w_ref.1), custom_call_target="tpu_custom_call" | custom-call | flops 35000000512 | bytes 146800640 | tf_op jit(solution)/shard_map/out_proj/pallas_call | solution.py:226
  296.6 3.1 %copy.31 = bf16[2,64,8192]{2,1,0:T(8,128)(2,1)} copy(bf16[2,64,8192]{2,1,0:T(8,128)(2,1)} %out_proj.1) | data formatting | bytes 4194304
  (8 shorter events, 0.1 us)
Async XLA Ops:
  6.3 1.6 copy-start
  7.9 1.2 copy-start.1
  188.8 1.9 copy-start.2

commit v3 on v2

v3 whole, which is shorter than its diff:
```python
import functools

import jax
import jax.numpy as jnp
from jax import lax
from jax.experimental import pallas as pl
from jax.experimental.pallas import tpu as pltpu
from jax.sharding import PartitionSpec as P

MESH = pl.DeviceIdType.MESH
CHUNK = 128
NB = 512
F32 = jnp.float32
BF16 = jnp.bfloat16


def silu(v):
    return v * jax.nn.sigmoid(v)


def ssd_step(g, chunk, tp, z_ref, x_ref, bc_ref, r_ref, cx_ref, nb_ref, hp_ref, bcs, q_out, xs, bs, xtail, btail, state, qs, prev):
    T = CHUNK
    width = xs.shape[1]
    n_state = bs.shape[1] // 2

    @pl.when(chunk == 0)
    def _():
        xtail[g] = jnp.zeros_like(xtail[g])
        btail[g] = jnp.zeros_like(btail[g])
        state[g] = jnp.zeros_like(state[g])

    xs[0:8, :] = xtail[g]
    bs[0:8, :] = btail[g]
    xs[8:8 + T, :] = x_ref[0].astype(F32)
    bs[8:8 + T, :] = bc_ref[0].astype(F32)
    xtail[g] = xs[T:T + 8, :]
    btail[g] = bs[T:T + 8, :]

    halves = []
    group = pl.ds(tp * 2 + g, 1)
    for c in range(2):
        lanes = slice(c * n_state, (c + 1) * n_state)
        conv = bcs[4, c, group, :]
        for tap in range(4):
            conv = conv + bs[5 + tap:5 + tap + T, lanes] * bcs[tap, c, group, :]
        halves.append(silu(conv).astype(BF16))
    b_mat, c_mat = halves
    scores = lax.dot_general(c_mat, b_mat, (((1,), (1,)), ((), ())), preferred_element_type=F32)
    b_t = jnp.transpose(b_mat.astype(F32)).astype(BF16)

    dt = jax.nn.softplus(r_ref[0].astype(F32) + hp_ref[0, 0:1, :])
    log_a = -jnp.exp(hp_ref[0, 1:2, :]) * dt
    row = lax.broadcasted_iota(jnp.int32, (T, T), 0)
    col = lax.broadcasted_iota(jnp.int32, (T, T), 1)
    causal = row >= col
    cum = jnp.dot(causal.astype(F32), log_a, preferred_element_type=F32, precision=lax.Precision.HIGHEST)
    cum_t = jnp.transpose(cum)
    dt_t = jnp.transpose(dt)
    left = lax.broadcasted_iota(jnp.int32, (T, 128), 1) < 64
    prev[...] = jnp.dot(c_mat, state[g].astype(BF16), preferred_element_type=F32)
    sq = jnp.zeros((T, 128), F32)

    for pair in range(width // 128):
        lanes = slice(pair * 128, pair * 128 + 128)
        conv = nb_ref[0:1, lanes].astype(F32)
        for tap in range(4):
            conv = conv + xs[5 + tap:5 + tap + T, lanes] * cx_ref[tap:tap + 1, lanes].astype(F32)
        u = silu(conv).astype(BF16)
        u32 = u.astype(F32)
        parts, cums, dts, skips = [], [], [], []
        for half in range(2):
            h = 2 * pair + half
            cum_b = jnp.broadcast_to(cum[:, h:h + 1], (T, 128))
            decay = jnp.exp(jnp.where(causal, cum_b - cum_t[h:h + 1, :], -1e30))
            w = scores * decay * dt_t[h:h + 1, :]
            parts.append(jnp.dot(w.astype(BF16), u, preferred_element_type=F32))
            cums.append(cum_b)
            dts.append(jnp.broadcast_to(dt[:, h:h + 1], (T, 128)))
            skips.append(jnp.broadcast_to(hp_ref[0, 2:3, h:h + 1], (1, 128)))
        cum_p = jnp.where(left, cums[0], cums[1])
        dt_p = jnp.where(left, dts[0], dts[1])
        skip = jnp.where(left[0:1], skips[0], skips[1])
        end = cum_p[T - 1:T, :]
        y = jnp.where(left, parts[0], parts[1]) + jnp.exp(cum_p) * prev[:, lanes] + skip * u32
        xw = (u32 * (jnp.exp(end - cum_p) * dt_p)).astype(BF16)
        state[g, :, lanes] = jnp.exp(end) * state[g, :, lanes] + jnp.dot(b_t, xw, preferred_element_type=F32)
        gated = y * silu(z_ref[0, :, lanes].astype(F32))
        qs[:, lanes] = gated
        sq = sq + gated * gated

    inv = lax.rsqrt(jnp.sum(sq, axis=1, keepdims=True) / width + 1e-5)
    cols = pl.ds(pl.multiple_of(g * width, width), width)
    q_out[lax.rem(chunk, 2), chunk // 2, :, cols] = (qs[...] * inv * nb_ref[1:2, :].astype(F32)).astype(BF16)


def scan_index(s, n_blk):
    return jnp.where(s < 4, s, jnp.where(s < 4 + n_blk, 4, jnp.minimum(s - n_blk, 7)))


def column_index(s, n_blk):
    first = jnp.where(s < 4, 0, s - 4)
    second = jnp.where(s < 8 + n_blk, 0, s - 8 - n_blk)
    last = s - 8 - 2 * n_blk
    return jnp.where(s < 4 + n_blk, first, jnp.where(s < 8 + 2 * n_blk, second, last))


def out_kernel(n_blk, rows, x_hbm, cbc_ref, bbc_ref, z_ref, x_ref, bc_ref, r_ref, cx_ref, nb_ref, hp_ref, w_ref, out_ref,
               res_ref, bcs, qv, xs, bs, xtail, btail, state, qs, prev, a1, rs1, rxx, a2, rs2, ysnd, yrx,
               lsem, s1, r1, s2, r2, sx, rx, sy, ry):
    s = pl.program_id(0)
    dp, sp, tp = lax.axis_index('dp'), lax.axis_index('sp'), lax.axis_index('tp')
    core = lax.rem(tp, 2)
    chip = tp // 2
    to_sib, to_x, to_y = (dp, sp, tp + 1 - 2 * core), (dp, sp, lax.rem(tp + 2, 4)), (dp, 1 - sp, tp)

    def res_copies():
        return [pltpu.make_async_copy(
            x_hbm.at[pl.ds(pl.multiple_of(blk * 4 * rows + tp * rows, rows), rows)],
            res_ref.at[blk], lsem.at[blk]) for blk in range(2)]

    def remote(src, dst, send_sem, recv_sem, peer):
        return pltpu.make_async_remote_copy(
            src_ref=src, dst_ref=dst, send_sem=send_sem, recv_sem=recv_sem, device_id=peer, device_id_type=MESH)

    def sib_first(h, m):
        return remote(a1.at[h, m, 1 - core], rs1.at[h, m], s1.at[h, m], r1.at[h, m], to_sib)

    def sib_second(m):
        return remote(a2.at[m, 1 - core], rs2.at[m], s2.at[m], r2.at[m], to_sib)

    def x_copy(h, m):
        return remote(a1.at[h, m, core], rxx.at[h, m], sx.at[h, m], rx.at[h, m], to_x)

    def y_copy(m):
        return remote(ysnd.at[m], yrx.at[m], sy.at[m], ry.at[m], to_y)

    @pl.when(s == 0)
    def _():
        for copy in res_copies():
            copy.start()
        barrier = pltpu.get_barrier_semaphore()
        for peer in (to_sib, to_x, to_y):
            pl.semaphore_signal(barrier, inc=1, device_id=peer, device_id_type=MESH)
        pl.semaphore_wait(barrier, 3)
        for copy in res_copies():
            copy.wait()
        for tap in range(4):
            bcs[tap] = cbc_ref[tap].astype(F32)
        bcs[4] = bbc_ref[...].astype(F32)

    def forward(h, m):
        sib_first(h, m).wait_recv()
        a1[h, m, core] = a1[h, m, core] + rs1[h, m]
        x_copy(h, m).start()

    @pl.when(s == 4 + n_blk)
    def _():
        forward(0, n_blk - 1)

    @pl.when(s == 8 + 2 * n_blk)
    def _():
        forward(1, n_blk - 1)

    scanning = jnp.logical_or(s < 4, jnp.logical_and(s >= 4 + n_blk, s < 8 + n_blk))

    @pl.when(scanning)
    def _():
        i = scan_index(s, n_blk)
        g = lax.rem(i, 4) // 2
        chunk = (i // 4) * 2 + lax.rem(i, 2)
        ssd_step(g, chunk, tp, z_ref, x_ref, bc_ref, r_ref, cx_ref, nb_ref, hp_ref, bcs, qv, xs, bs, xtail, btail, state, qs, prev)

    @pl.when(jnp.logical_and(jnp.logical_not(scanning), s < 8 + 2 * n_blk))
    def _():
        n = column_index(s, n_blk)
        h = jnp.where(s < 4 + n_blk, 0, 1)
        acc = jnp.dot(qv[1 - chip, h], w_ref[...], preferred_element_type=F32)
        a1[h, n, 0] = acc[:rows]
        a1[h, n, 1] = acc[rows:]
        sib_first(h, n).start()

        @pl.when(n >= 1)
        def _():
            forward(h, n - 1)

    @pl.when(s >= 8 + 2 * n_blk)
    def _():
        n = column_index(s, n_blk)
        acc = jnp.dot(qv[chip].reshape(4 * rows, qv.shape[3]), w_ref[...], preferred_element_type=F32)
        for h in range(2):
            for c in range(2):
                a2[n, c, h] = acc[(2 * h + c) * rows:(2 * h + c + 1) * rows]
        sib_second(n).start()

    @pl.when(s == 7 + 3 * n_blk)
    def _():
        for h in range(2):
            def finish(m, carry):
                if h == 0:
                    sib_second(m).wait_recv()
                x_copy(h, m).wait_recv()
                cols = pl.ds(pl.multiple_of(m * NB, NB), NB)
                total = a2[m, core, h] + rs2[m, h] + rxx[h, m] + res_ref[h, :, cols].astype(F32)

                @pl.when(sp == h)
                def _():
                    out_ref[h, :, cols] = total.astype(BF16)

                @pl.when(sp != h)
                def _():
                    ysnd[m] = total.astype(BF16)
                    y_copy(m).start()

                return carry

            lax.fori_loop(0, n_blk, finish, 0)

        def drain(m, carry):
            y_copy(m).wait_recv()
            cols = pl.ds(pl.multiple_of(m * NB, NB), NB)
            out_ref[1 - sp, :, cols] = yrx[m]
            for h in range(2):
                sib_first(h, m).wait_send()
                x_copy(h, m).wait_send()
            sib_second(m).wait_send()
            y_copy(m).wait_send()
            return carry

        lax.fori_loop(0, n_blk, drain, 0)


def out_call(x_all, zx, bc, r, conv_x, conv_bc, bias_bc, nb, hp, w_out, rows):
    depth, d_model = w_out.shape
    n_blk = d_model // NB
    inner = zx.shape[2]
    groups = bc.shape[0]
    width = inner // groups
    n_bc = bc.shape[2]
    T = CHUNK
    dma = pltpu.SemaphoreType.DMA

    def at(make):
        def index(s):
            i = scan_index(s, n_blk)
            return make(lax.rem(i, 4) // 2, (i // 4) * 2 + lax.rem(i, 2))
        return index

    vmem = pl.BlockSpec(memory_space=pltpu.VMEM)
    return pl.pallas_call(
        functools.partial(out_kernel, n_blk, rows),
        grid=(8 + 3 * n_blk,),
        in_specs=[
            pl.BlockSpec(memory_space=pl.ANY),
            vmem,
            vmem,
            pl.BlockSpec((1, T, width), at(lambda g, c: (0, c, g))),
            pl.BlockSpec((1, T, width), at(lambda g, c: (1, c, g))),
            pl.BlockSpec((1, T, n_bc), at(lambda g, c: (g, c, 0))),
            pl.BlockSpec((1, T, 128), at(lambda g, c: (g, c, 0))),
            pl.BlockSpec((4, width), at(lambda g, c: (0, g))),
            pl.BlockSpec((2, width), at(lambda g, c: (0, g))),
            pl.BlockSpec((1, 3, 128), at(lambda g, c: (g, 0, 0))),
            pl.BlockSpec((depth, NB), lambda s: (0, column_index(s, n_blk))),
        ],
        out_specs=vmem,
        out_shape=jax.ShapeDtypeStruct((2, rows, d_model), BF16),
        scratch_shapes=[
            pltpu.VMEM((2, rows, d_model), BF16),
            pltpu.VMEM((5,) + conv_bc.shape[1:], F32),
            pltpu.VMEM((2, 2, T, inner), BF16),
            pltpu.VMEM((T + 8, width), F32),
            pltpu.VMEM((T + 8, n_bc), F32),
            pltpu.VMEM((groups, 8, width), F32),
            pltpu.VMEM((groups, 8, n_bc), F32),
            pltpu.VMEM((groups, n_bc // 2, width), F32),
            pltpu.VMEM((T, width), F32),
            pltpu.VMEM((T, width), F32),
            pltpu.VMEM((2, n_blk, 2, rows, NB), F32),
            pltpu.VMEM((2, n_blk, rows, NB), F32),
            pltpu.VMEM((2, n_blk, rows, NB), F32),
            pltpu.VMEM((n_blk, 2, 2, rows, NB), F32),
            pltpu.VMEM((n_blk, 2, rows, NB), F32),
            pltpu.VMEM((n_blk, rows, NB), BF16),
            pltpu.VMEM((n_blk, rows, NB), BF16),
            dma((2,)), dma((2, n_blk)), dma((2, n_blk)), dma((n_blk,)), dma((n_blk,)),
            dma((2, n_blk)), dma((2, n_blk)), dma((n_blk,)), dma((n_blk,)),
        ],
        compiler_params=pltpu.CompilerParams(
            dimension_semantics=('arbitrary',), collective_id=1, has_side_effects=True, vmem_limit_bytes=67043328),
        cost_estimate=pl.CostEstimate(flops=43 * 10**9, bytes_accessed=220 * 2**20, transcendentals=10**7),
        name='scan_out',
    )(x_all, conv_bc, bias_bc, zx, zx, bc, r, conv_x, nb, hp, w_out)


def gather_kernel(n_chunk, x_hbm, w_ref, wdt_ref, xall_ref, bc_ref, r_ref, xg, wv, acc, racc, lsem, wsem, osem, ss, rs):
    dp, sp, tp = lax.axis_index('dp'), lax.axis_index('sp'), lax.axis_index('tp')
    rows = x_hbm.shape[1]
    width = xg.shape[2]
    half = width // 2
    core = lax.rem(tp, 2)
    sib = tp + 1 - 2 * core
    across = lax.rem(tp + 2, 4)
    diag = lax.rem(sib + 2, 4)
    to_sib, to_x, to_y = (dp, sp, sib), (dp, sp, across), (dp, 1 - sp, tp)

    def slot(k, blk, owner):
        return xg.at[k, pl.ds(pl.multiple_of((blk * 4 + owner) * rows, rows), rows)]

    def columns(seq, k):
        return x_hbm.at[seq, :, pl.ds(k * width, width)]

    def local(k):
        return pltpu.make_async_copy(columns(sp, k), slot(k, sp, tp), lsem.at[k])

    def weights(k):
        return [pltpu.make_async_copy(
            w_ref.at[pl.ds(k * half, half), par, c, j, tp], wv.at[k, par, c, j], wsem.at[k, par * 4 + c * 2 + j])
            for par in range(2) for c in range(2) for j in range(2)]

    def send(kind, k):
        source, target = [
            (None, to_y),
            ((sp, tp), to_x), ((1 - sp, tp), to_x),
            ((sp, tp), to_sib), ((1 - sp, tp), to_sib),
            ((sp, across), to_sib), ((1 - sp, across), to_sib),
        ][kind]
        if source is None:
            src, dst = columns(1 - sp, k), slot(k, sp, tp)
        else:
            src = dst = slot(k, *source)
        return pltpu.make_async_remote_copy(
            src_ref=src, dst_ref=dst, send_sem=ss.at[kind, k], recv_sem=rs.at[kind, k],
            device_id=target, device_id_type=MESH)

    def arrived(kind, k):
        blk, owner = [(1 - sp, tp), (sp, across), (1 - sp, across), (sp, sib), (1 - sp, sib), (sp, diag), (1 - sp, diag)][kind]
        here = slot(k, blk, owner)
        pltpu.make_async_remote_copy(
            src_ref=here, dst_ref=here, send_sem=ss.at[kind, k], recv_sem=rs.at[kind, k],
            device_id=to_sib, device_id_type=MESH).wait_recv()

    def store(k):
        return pltpu.make_async_copy(xg.at[k], xall_ref.at[:, pl.ds(k * width, width)], osem.at[k])

    for k in range(n_chunk):
        local(k).start()
    for k in range(n_chunk):
        for copy in weights(k):
            copy.start()
    barrier = pltpu.get_barrier_semaphore()
    for peer in (to_sib, to_x, to_y):
        pl.semaphore_signal(barrier, inc=1, device_id=peer, device_id_type=MESH)
    pl.semaphore_wait(barrier, 3)

    def own_out(k):
        local(k).wait()
        send(1, k).start()
        send(3, k).start()

    def swapped_out(k):
        arrived(0, k)
        send(2, k).start()
        send(4, k).start()

    step = 512
    even = lax.rem(lax.broadcasted_iota(jnp.int32, (step // 8, 8, 128), 1), 2) == 0

    def compute(k):
        arrived(1, k)
        send(5, k).start()
        arrived(2, k)
        send(6, k).start()
        for copy in weights(k):
            copy.wait()
        for kind in range(3, 7):
            arrived(kind, k)
        store(k).start()

        def part(i, carry):
            span = pl.ds(pl.multiple_of(i * step, step), step)
            lhs = xg[k, :, span]
            for c in range(2):
                first, second = [], []
                for j in range(2):
                    a = wv.at[k, 0, c, j].reshape(width, 128)[span, :].astype(F32).reshape(step // 8, 8, 128)
                    b = wv.at[k, 1, c, j].reshape(width, 128)[span, :].astype(F32).reshape(step // 8, 8, 128)
                    first.append(jnp.where(even, a, pltpu.roll(b, 1, 1)).reshape(step, 128).astype(BF16))
                    second.append(jnp.where(even, pltpu.roll(a, 7, 1), b).reshape(step, 128).astype(BF16))
                for g, pieces in enumerate((first, second)):
                    acc[g, c] += jnp.dot(lhs, jnp.concatenate(pieces, axis=1), preferred_element_type=F32)
            return carry

        lax.fori_loop(0, width // step, part, 0)
        racc[...] += lax.dot_general(
            xg[k], wdt_ref[:, k * width:(k + 1) * width], (((1,), (1,)), ((), ())), preferred_element_type=F32)

    for k in range(n_chunk):
        send(0, k).start()
    acc[...] = jnp.zeros_like(acc)
    racc[...] = jnp.zeros_like(racc)
    own_out(0)
    own_out(1)
    swapped_out(0)
    own_out(2)
    swapped_out(1)
    own_out(3)
    compute(0)
    swapped_out(2)
    compute(1)
    swapped_out(3)
    compute(2)
    compute(3)

    for g in range(2):
        for c in range(2):
            bc_ref[g, :, c * 256:(c + 1) * 256] = acc[g, c].astype(BF16)
    per_group = racc.shape[1] // 2
    r_ref[...] = jnp.zeros_like(r_ref)
    for g in range(2):
        r_ref[g, :, 0:per_group] = racc[:, g * per_group:(g + 1) * per_group].astype(BF16)
    for k in range(n_chunk):
        for kind in range(7):
            send(kind, k).wait_send()
        store(k).wait()


def gather_call(x_loc, w_bc, w_dt):
    n_seq, rows, d_model = x_loc.shape
    n_tok = 8 * rows
    n_chunk = 4
    width = d_model // n_chunk
    heads = w_dt.shape[1]
    w_view = w_bc.reshape(d_model // 2, 2, 2, 4, 2, 2, 128).transpose(0, 1, 2, 5, 3, 4, 6)
    anywhere = pl.BlockSpec(memory_space=pl.ANY)
    vmem = pl.BlockSpec(memory_space=pltpu.VMEM)
    dma = pltpu.SemaphoreType.DMA
    return pl.pallas_call(
        functools.partial(gather_kernel, n_chunk),
        in_specs=[anywhere, anywhere, vmem],
        out_specs=(anywhere, vmem, vmem),
        out_shape=(
            jax.ShapeDtypeStruct((n_tok, d_model), BF16),
            jax.ShapeDtypeStruct((2, n_tok, 512), BF16),
            jax.ShapeDtypeStruct((2, n_tok, 128), BF16),
        ),
        scratch_shapes=[
            pltpu.VMEM((n_chunk, n_tok, width), BF16),
            pltpu.VMEM((n_chunk, 2, 2, 2, width // 2, 2, 128), BF16),
            pltpu.VMEM((2, 2, n_tok, 256), F32),
            pltpu.VMEM((n_tok, heads), F32),
            dma((n_chunk,)), dma((n_chunk, 8)), dma((n_chunk,)), dma((7, n_chunk)), dma((7, n_chunk)),
        ],
        compiler_params=pltpu.CompilerParams(collective_id=2, has_side_effects=True, vmem_limit_bytes=48 * 2**20),
        cost_estimate=pl.CostEstimate(flops=10**10, bytes_accessed=30 * 2**20, transcendentals=0),
        name='gather_bc',
    )(x_loc, w_view, w_dt.T)


def solution(mesh):
    tp_size = mesh.shape['tp']
    tok_spec = P('dp', ('sp', 'tp'), None)

    def local_layer(x_loc, w_zx, w_dt, w_bc, conv_x, conv_bc, bias_x, bias_bc, a_log, dt_bias, d_skip, norm_w, w_out):
        rows = x_loc.shape[1]
        g_loc = w_bc.shape[2] // tp_size
        x_all, bc, r = gather_call(x_loc, w_bc, w_dt)
        zx = jnp.einsum('md,dcn->cmn', x_all, w_zx, preferred_element_type=F32).astype(BF16)
        hp = jnp.stack([dt_bias.reshape(g_loc, -1), a_log.reshape(g_loc, -1), d_skip.reshape(g_loc, -1)], axis=1)
        hp = jnp.pad(hp, ((0, 0), (0, 0), (0, 128 - hp.shape[2])))
        nb = jnp.stack([bias_x, norm_w])
        return out_call(x_all, zx, bc, r, conv_x, conv_bc, bias_bc, nb, hp, w_out, rows)

    in_specs = (tok_spec, P(None, None, 'tp'), P(None, 'tp'), P(), P(None, 'tp'), P(), P('tp'), P(), P('tp'), P('tp'), P('tp'), P('tp'), P('tp', None))
    return jax.shard_map(local_layer, mesh=mesh, in_specs=in_specs, out_specs=tok_spec, check_vma=False)
```

time: 301 us -> 306 us (1.017)
  Pallas kernels: 197 us -> 204 us
    pallas_call x2 -> x1, Pallas kernels: 136 us -> 143 us  [out_call(): pl.pallas_call(functools.partial(out_kernel, n_blk, rows), grid=(8 + 3 *...]
    unnamed x7 -> x9, local copies, waits for them, and re-layouts: 7.85 us -> 7.58 us
where the time goes in v3:
time: 306 us; the launch traced here: 304 us
  Pallas kernels  204 us (67%)
  matrix products  88.3 us (29%)
  local copies, waits for them, and re-layouts  11.2 us (4%)
    pallas_call x1, Pallas kernels, out_call(): pl.pallas_call(functools.partial(out_kernel, n_blk, rows), grid=(8 + 3 *...  143 us
    dot_general x1, matrix products, local_layer(): jnp.einsum('md,dcn->cmn', x_all, w_zx, preferred_element_type=F32)  88.3 us
    pallas_call x1, Pallas kernels, gather_call(): pl.pallas_call(functools.partial(gather_kernel, n_chunk), in_specs=[anywh...  60.7 us
    unnamed x9, local copies, waits for them, and re-layouts  7.58 us

profile of v3, /device:TPU:0, one launch (start us, length us, event | category | flops | bytes accessed | tf_op | source)
XLA Modules:
  0.0 304.4 jit_solution(7760901750505146969)
XLA Ops:
  0.0 0.7 stack_reshape.10
  0.7 0.7 stack_reshape.9
  1.5 0.7 stack_reshape.11
  2.2 0.6 select_maximum_fusion.hp_ref
  2.8 0.7 stack.12
  3.5 0.7 stack.13
  4.2 0.6 pad_maximum_fusion.nb_ref
  4.9 0.0 copy-start
  4.9 1.6 copy-done
  6.5 0.0 copy-start.1
  6.5 1.2 copy-done.1
  7.7 60.7 %gather_bc.1 = (bf16[512,8192]{1,0:T(8,128)(2,1)}, bf16[2,512,512]{2,1,0:T(8,128)(2,1)S(1)}, bf16[2,512,128]{2,1,0:T(8,128)(2,1)S(1)}) custom-call(bf16[2,64,8192]{2,1,0:T(8,128)(2,1)S(1)} %copy-done, bf16[4096,2,2,2,4,2,128]{6,5,4,3,2,1,0:T(2,128)(2,1)} %bitcast.1.w_ref, bf16[64,8192]{1,0:T(8,128)(2,1)S(1)} %bitcast.14), custom_call_target="tpu_custom_call" | custom-call | flops 10000000000 | bytes 31457280 | tf_op jit(solution)/shard_map/gather_bc/pallas_call | solution.py:437
  68.4 0.0 copy-start.2
  68.4 1.0 copy-done.2
  69.4 0.0 copy-start.3
  69.4 0.7 copy-done.3
  70.1 88.3 %convert_bitcast_fusion.z_ref.x_ref = bf16[2,512,4096]{2,1,0:T(8,128)(2,1)} fusion(bf16[8192,2,4096]{2,1,0:T(2,128)(2,1)} %param.14, bf16[512,8192]{1,0:T(8,128)(2,1)} %get-tuple-element.8.x_hbm), kind=kOutput, calls=%fused_computation.3 | convolution fusion | flops 68723671040 | bytes 150994944 | tf_op jit(solution)/shard_map/md,dcn->cmn/dot_general | solution.py:467
  158.4 142.9 %scan_out.1 = bf16[2,64,8192]{2,1,0:T(8,128)(2,1)} custom-call(bf16[512,8192]{1,0:T(8,128)(2,1)} %get-tuple-element.8.x_hbm, bf16[4,2,8,256]{3,2,1,0:T(8,128)(2,1)} %cbc_ref.1, bf16[2,8,256]{2,1,0:T(8,128)(2,1)} %bbc_ref.1, bf16[2,512,4096]{2,1,0:T(8,128)(2,1)} %convert_bitcast_fusion.z_ref.x_ref, bf16[2,512,4096]{2,1,0:T(8,128)(2,1)} %convert_bitcast_fusion.z_ref.x_ref, ...), custom_call_target="tpu_custom_call" | custom-call | flops 43000000512 | bytes 230686720 | tf_op jit(solution)/shard_map/scan_out/pallas_call | solution.py:249
  301.3 3.1 %copy.23 = bf16[2,64,8192]{2,1,0:T(8,128)(2,1)} copy(bf16[2,64,8192]{2,1,0:T(8,128)(2,1)} %scan_out.1) | data formatting | bytes 4194304
Async XLA Ops:
  4.9 1.6 copy-start
  6.5 1.2 copy-start.1
  68.4 1.0 copy-start.2
  69.4 0.7 copy-start.3

commit v4 on v3

--- a/solution.py
+++ b/solution.py
@@ -90,7 +90,7 @@
 
     inv = lax.rsqrt(jnp.sum(sq, axis=1, keepdims=True) / width + 1e-5)
     cols = pl.ds(pl.multiple_of(g * width, width), width)
-    q_out[lax.rem(chunk, 2), chunk // 2, :, cols] = (qs[...] * inv * nb_ref[1:2, :].astype(F32)).astype(BF16)
+    q_out[chunk // 2, lax.rem(chunk, 2), :, cols] = (qs[...] * inv * nb_ref[1:2, :].astype(F32)).astype(BF16)
 
 
 def scan_index(s, n_blk):
@@ -98,14 +98,11 @@
 
 
 def column_index(s, n_blk):
-    first = jnp.where(s < 4, 0, s - 4)
-    second = jnp.where(s < 8 + n_blk, 0, s - 8 - n_blk)
-    last = s - 8 - 2 * n_blk
-    return jnp.where(s < 4 + n_blk, first, jnp.where(s < 8 + 2 * n_blk, second, last))
+    return jnp.where(s < 4 + n_blk, jnp.maximum(s - 4, 0), jnp.maximum(s - 8 - n_blk, 0))
 
 
 def out_kernel(n_blk, rows, x_hbm, cbc_ref, bbc_ref, z_ref, x_ref, bc_ref, r_ref, cx_ref, nb_ref, hp_ref, w_ref, out_ref,
-               res_ref, bcs, qv, xs, bs, xtail, btail, state, qs, prev, a1, rs1, rxx, a2, rs2, ysnd, yrx,
+               res_ref, bcs, qv, xs, bs, xtail, btail, state, qs, prev, ab, rs1, rxx, rs2, ysnd, yrx,
                lsem, s1, r1, s2, r2, sx, rx, sy, ry):
     s = pl.program_id(0)
     dp, sp, tp = lax.axis_index('dp'), lax.axis_index('sp'), lax.axis_index('tp')
@@ -123,13 +120,13 @@
             src_ref=src, dst_ref=dst, send_sem=send_sem, recv_sem=recv_sem, device_id=peer, device_id_type=MESH)
 
     def sib_first(h, m):
-        return remote(a1.at[h, m, 1 - core], rs1.at[h, m], s1.at[h, m], r1.at[h, m], to_sib)
-
-    def sib_second(m):
-        return remote(a2.at[m, 1 - core], rs2.at[m], s2.at[m], r2.at[m], to_sib)
+        return remote(ab.at[h, m, 1 - chip, 1 - core], rs1.at[h, m], s1.at[h, m], r1.at[h, m], to_sib)
+
+    def sib_second(h, m):
+        return remote(ab.at[h, m, chip, 1 - core], rs2.at[h, m], s2.at[h, m], r2.at[h, m], to_sib)
 
     def x_copy(h, m):
-        return remote(a1.at[h, m, core], rxx.at[h, m], sx.at[h, m], rx.at[h, m], to_x)
+        return remote(ab.at[h, m, 1 - chip, core], rxx.at[h, m], sx.at[h, m], rx.at[h, m], to_x)
 
     def y_copy(m):
         return remote(ysnd.at[m], yrx.at[m], sy.at[m], ry.at[m], to_y)
@@ -150,16 +147,12 @@
 
     def forward(h, m):
         sib_first(h, m).wait_recv()
-        a1[h, m, core] = a1[h, m, core] + rs1[h, m]
+        ab[h, m, 1 - chip, core] = ab[h, m, 1 - chip, core] + rs1[h, m]
         x_copy(h, m).start()
 
     @pl.when(s == 4 + n_blk)
     def _():
         forward(0, n_blk - 1)
-
-    @pl.when(s == 8 + 2 * n_blk)
-    def _():
-        forward(1, n_blk - 1)
 
     scanning = jnp.logical_or(s < 4, jnp.logical_and(s >= 4 + n_blk, s < 8 + n_blk))
 
@@ -170,37 +163,29 @@
         chunk = (i // 4) * 2 + lax.rem(i, 2)
         ssd_step(g, chunk, tp, z_ref, x_ref, bc_ref, r_ref, cx_ref, nb_ref, hp_ref, bcs, qv, xs, bs, xtail, btail, state, qs, prev)
 
-    @pl.when(jnp.logical_and(jnp.logical_not(scanning), s < 8 + 2 * n_blk))
+    @pl.when(jnp.logical_not(scanning))
     def _():
         n = column_index(s, n_blk)
         h = jnp.where(s < 4 + n_blk, 0, 1)
-        acc = jnp.dot(qv[1 - chip, h], w_ref[...], preferred_element_type=F32)
-        a1[h, n, 0] = acc[:rows]
-        a1[h, n, 1] = acc[rows:]
+        acc = jnp.dot(qv[h].reshape(4 * rows, qv.shape[3]), w_ref[...], preferred_element_type=F32)
+        for i in range(4):
+            ab[h, n, i // 2, i % 2] = acc[i * rows:(i + 1) * rows]
         sib_first(h, n).start()
+        sib_second(h, n).start()
 
         @pl.when(n >= 1)
         def _():
             forward(h, n - 1)
 
-    @pl.when(s >= 8 + 2 * n_blk)
-    def _():
-        n = column_index(s, n_blk)
-        acc = jnp.dot(qv[chip].reshape(4 * rows, qv.shape[3]), w_ref[...], preferred_element_type=F32)
-        for h in range(2):
-            for c in range(2):
-                a2[n, c, h] = acc[(2 * h + c) * rows:(2 * h + c + 1) * rows]
-        sib_second(n).start()
-
-    @pl.when(s == 7 + 3 * n_blk)
-    def _():
+    @pl.when(s == 7 + 2 * n_blk)
+    def _():
+        forward(1, n_blk - 1)
         for h in range(2):
             def finish(m, carry):
-                if h == 0:
-                    sib_second(m).wait_recv()
+                sib_second(h, m).wait_recv()
                 x_copy(h, m).wait_recv()
                 cols = pl.ds(pl.multiple_of(m * NB, NB), NB)
-                total = a2[m, core, h] + rs2[m, h] + rxx[h, m] + res_ref[h, :, cols].astype(F32)
+                total = ab[h, m, chip, core] + rs2[h, m] + rxx[h, m] + res_ref[h, :, cols].astype(F32)
 
                 @pl.when(sp == h)
                 def _():
@@ -222,7 +207,7 @@
             for h in range(2):
                 sib_first(h, m).wait_send()
                 x_copy(h, m).wait_send()
-            sib_second(m).wait_send()
+                sib_second(h, m).wait_send()
             y_copy(m).wait_send()
             return carry
 
@@ -248,7 +233,7 @@
     vmem = pl.BlockSpec(memory_space=pltpu.VMEM)
     return pl.pallas_call(
         functools.partial(out_kernel, n_blk, rows),
-        grid=(8 + 3 * n_blk,),
+        grid=(8 + 2 * n_blk,),
         in_specs=[
             pl.BlockSpec(memory_space=pl.ANY),
             vmem,
@@ -275,14 +260,13 @@
             pltpu.VMEM((groups, n_bc // 2, width), F32),
             pltpu.VMEM((T, width), F32),
             pltpu.VMEM((T, width), F32),
-            pltpu.VMEM((2, n_blk, 2, rows, NB), F32),
+            pltpu.VMEM((2, n_blk, 2, 2, rows, NB), F32),
             pltpu.VMEM((2, n_blk, rows, NB), F32),
             pltpu.VMEM((2, n_blk, rows, NB), F32),
-            pltpu.VMEM((n_blk, 2, 2, rows, NB), F32),
-            pltpu.VMEM((n_blk, 2, rows, NB), F32),
+            pltpu.VMEM((2, n_blk, rows, NB), F32),
             pltpu.VMEM((n_blk, rows, NB), BF16),
             pltpu.VMEM((n_blk, rows, NB), BF16),
-            dma((2,)), dma((2, n_blk)), dma((2, n_blk)), dma((n_blk,)), dma((n_blk,)),
+            dma((2,)), dma((2, n_blk)), dma((2, n_blk)), dma((2, n_blk)), dma((2, n_blk)),
             dma((2, n_blk)), dma((2, n_blk)), dma((n_blk,)), dma((n_blk,)),
         ],
         compiler_params=pltpu.CompilerParams(

time: 306 us -> 283 us (0.925)
  Pallas kernels: 204 us -> 181 us
    pallas_call x1, Pallas kernels: 143 us -> 121 us  [out_call(): pl.pallas_call(functools.partial(out_kernel, n_blk, rows), grid=(8 + 2 *...]
where the time goes in v4:
time: 283 us; the launch traced here: 282 us
  Pallas kernels  181 us (64%)
  matrix products  88.3 us (31%)
  local copies, waits for them, and re-layouts  11.2 us (4%)
    pallas_call x1, Pallas kernels, out_call(): pl.pallas_call(functools.partial(out_kernel, n_blk, rows), grid=(8 + 2 *...  121 us
    dot_general x1, matrix products, local_layer(): jnp.einsum('md,dcn->cmn', x_all, w_zx, preferred_element_type=F32)  88.3 us
    pallas_call x1, Pallas kernels, gather_call(): pl.pallas_call(functools.partial(gather_kernel, n_chunk), in_specs=[anywh...  60.7 us
    unnamed x9, local copies, waits for them, and re-layouts  7.58 us

profile of v4, /device:TPU:0, one launch (start us, length us, event | category | flops | bytes accessed | tf_op | source)
XLA Modules:
  0.0 282.1 jit_solution(6307498547787557117)
XLA Ops:
  0.0 0.7 stack_reshape.10
  0.7 0.7 stack_reshape.9
  1.5 0.7 stack_reshape.11
  2.2 0.6 select_maximum_fusion.hp_ref
  2.8 0.7 stack.12
  3.5 0.7 stack.13
  4.2 0.6 pad_maximum_fusion.nb_ref
  4.9 0.0 copy-start
  4.9 1.6 copy-done
  6.5 0.0 copy-start.1
  6.5 1.2 copy-done.1
  7.7 60.7 %gather_bc.1 = (bf16[512,8192]{1,0:T(8,128)(2,1)}, bf16[2,512,512]{2,1,0:T(8,128)(2,1)S(1)}, bf16[2,512,128]{2,1,0:T(8,128)(2,1)S(1)}) custom-call(bf16[2,64,8192]{2,1,0:T(8,128)(2,1)S(1)} %copy-done, bf16[4096,2,2,2,4,2,128]{6,5,4,3,2,1,0:T(2,128)(2,1)} %bitcast.1.w_ref, bf16[64,8192]{1,0:T(8,128)(2,1)S(1)} %bitcast.14), custom_call_target="tpu_custom_call" | custom-call | flops 10000000000 | bytes 31457280 | tf_op jit(solution)/shard_map/gather_bc/pallas_call | solution.py:421
  68.4 0.0 copy-start.2
  68.4 1.0 copy-done.2
  69.4 0.0 copy-start.3
  69.4 0.7 copy-done.3
  70.1 88.3 %convert_bitcast_fusion.z_ref.x_ref = bf16[2,512,4096]{2,1,0:T(8,128)(2,1)} fusion(bf16[8192,2,4096]{2,1,0:T(2,128)(2,1)} %param.14, bf16[512,8192]{1,0:T(8,128)(2,1)} %get-tuple-element.8.x_hbm), kind=kOutput, calls=%fused_computation.3 | convolution fusion | flops 68723671040 | bytes 150994944 | tf_op jit(solution)/shard_map/md,dcn->cmn/dot_general | solution.py:451
  158.4 120.6 %scan_out.1 = bf16[2,64,8192]{2,1,0:T(8,128)(2,1)} custom-call(bf16[512,8192]{1,0:T(8,128)(2,1)} %get-tuple-element.8.x_hbm, bf16[4,2,8,256]{3,2,1,0:T(8,128)(2,1)} %cbc_ref.1, bf16[2,8,256]{2,1,0:T(8,128)(2,1)} %bbc_ref.1, bf16[2,512,4096]{2,1,0:T(8,128)(2,1)} %convert_bitcast_fusion.z_ref.x_ref, bf16[2,512,4096]{2,1,0:T(8,128)(2,1)} %convert_bitcast_fusion.z_ref.x_ref, ...), custom_call_target="tpu_custom_call" | custom-call | flops 43000000512 | bytes 230686720 | tf_op jit(solution)/shard_map/scan_out/pallas_call | solution.py:234
  279.0 3.1 %copy.23 = bf16[2,64,8192]{2,1,0:T(8,128)(2,1)} copy(bf16[2,64,8192]{2,1,0:T(8,128)(2,1)} %scan_out.1) | data formatting | bytes 4194304
Async XLA Ops:
  4.9 1.6 copy-start
  6.5 1.2 copy-start.1
  68.4 1.0 copy-start.2
  69.4 0.7 copy-start.3
